TPU v7x, 32 devices: a whole 2x2x4 slice. The times are simulated.
32 devices in a mesh: fsdp: 8 (over y, x, core), tensor: 4 (over z).
Axes of the slice: x: 2, y: 2, z: 4, core: 2. Of those that a mesh axis runs over, the one named last changes fastest.
Arguments:
- new_hidden: bfloat16 [128, 2, 8192], P('fsdp'), may hold values from -6 to 6
- new_queries: bfloat16 [128, 2, 8192], P('fsdp', None, 'tensor'), may hold values from -540 to 540
- paged_cache: bfloat16 [256, 64, 2048], P('fsdp', None, 'tensor'), may hold values from -6 to 6
- block_table: int32 [128, 8], P('fsdp'), may hold values from 0 to 31
- lengths: int32 [128], P('fsdp'), may hold values from 1 to 512
- destination: int32 [128], P('fsdp'), may hold values from -1 to 7, as said below
- train_hidden: bfloat16 [512, 8192], P('fsdp'), may hold values from -6 to 6
- train_queries: bfloat16 [512, 8192], P('fsdp', 'tensor'), may hold values from -540 to 540
- documents: int32 [8, 64], P('fsdp'), may hold values from 0 to 3, never falling along the last dimension, each value on 1 to 32 neighbouring positions
- project_weight: bfloat16 [8192, 2048], P('fsdp', 'tensor'), may hold values from -0.0625 to 0.0625
- project_bias: float32 [2048], P('tensor'), may hold values from -3 to 3
Outputs:
- decoded: bfloat16 [128, 2, 8192], P('fsdp', None, 'tensor')
- train_attention: bfloat16 [512, 8192], P('fsdp', 'tensor')
- handover: bfloat16 [64, 2, 2048], P('fsdp', None, 'tensor')
Inputs may be any that keep to these rules, and one draw needn't show every extreme that they name: `destination`: the rows of one fsdp index name each training shard at most once.
All inputs are finite; a program needn't handle non-finite values.
Results may differ from a plain program's by a relative error of at most 0.0095.
Values may be sent and summed in bfloat16 or wider, within the bound.
No kernel may reach another device: no remote copies, remote signals or barrier semaphores. Data moves between devices by JAX's collectives and lax.ppermute only.
A program may use at most 64 MiB of HBM per device.

v0:
```python
import jax
import jax.numpy as jnp
from jax import lax
from jax.sharding import PartitionSpec as P

HEADS = 64
KV_HEADS = 8
HEAD_DIM = 128


masked_value = -1e30


def local(
    new_hidden,
    new_queries,
    paged_cache,
    block_table,
    lengths,
    destination,
    train_hidden,
    train_queries,
    documents,
    project_weight,
    project_bias,
):
    row_count = new_hidden.shape[0]
    model_width = new_hidden.shape[2]
    columns = project_weight.shape[1]
    local_kv = columns // (2 * HEAD_DIM)
    group_size = HEADS // KV_HEADS
    scaling = HEAD_DIM ** (-0.5)
    train_count = train_hidden.shape[0]
    flat_new = new_hidden.reshape(row_count * 2, model_width)
    gathered = lax.all_gather(project_weight, "fsdp", axis=0, tiled=True)
    decode_sum = jnp.dot(flat_new, gathered, preferred_element_type=jnp.float32)
    train_sum = jnp.dot(train_hidden, gathered, preferred_element_type=jnp.float32)
    fresh = (
        (decode_sum + project_bias)
        .astype(jnp.bfloat16)
        .reshape(row_count, 2, local_kv, 2, HEAD_DIM)
    )
    train_kv = (
        (train_sum + project_bias).astype(jnp.bfloat16).reshape(train_count, local_kv, 2, HEAD_DIM)
    )
    owners = lax.axis_size("fsdp")
    selector = (destination[None, :] == jnp.arange(owners, dtype=jnp.int32)[:, None]).astype(
        jnp.bfloat16
    )
    outgoing = jnp.dot(
        selector, fresh.reshape(row_count, 2 * columns), preferred_element_type=jnp.float32
    )
    outgoing = outgoing.astype(jnp.bfloat16).reshape(owners, 2, columns)
    handover = lax.all_to_all(outgoing, "fsdp", split_axis=0, concat_axis=0, tiled=True)
    context = paged_cache.shape[1] * block_table.shape[1]
    block_rows = 16
    count_blocks = row_count // block_rows
    order = jnp.arange(2, dtype=jnp.int32)
    allowed_new = order[None, :] <= order[:, None]
    places = jnp.arange(context, dtype=jnp.int32)

    def decode_block(operands):
        queries, tables, spans, fresh_rows = operands
        cached = jnp.take(paged_cache, tables, axis=0).reshape(
            block_rows, context, local_kv, 2, HEAD_DIM
        )
        heads_q = queries.reshape(block_rows, 2, local_kv, group_size, HEAD_DIM)
        old_scores = (
            jnp.einsum(
                "btkgd,bckd->btkgc",
                heads_q,
                cached[:, :, :, 0, :],
                preferred_element_type=jnp.float32,
            )
            * scaling
        )
        allowed_old = places[None, :] < spans[:, None]
        old_scores = jnp.where(allowed_old[:, None, None, None, :], old_scores, masked_value)
        new_scores = (
            jnp.einsum(
                "btkgd,bskd->btkgs",
                heads_q,
                fresh_rows[:, :, :, 0, :],
                preferred_element_type=jnp.float32,
            )
            * scaling
        )
        new_scores = jnp.where(allowed_new[None, :, None, None, :], new_scores, masked_value)
        highest = jnp.maximum(
            jnp.max(old_scores, -1, keepdims=True), jnp.max(new_scores, -1, keepdims=True)
        )
        old_exp = jnp.exp(old_scores - highest)
        new_exp = jnp.exp(new_scores - highest)
        totals = jnp.sum(old_exp, -1, keepdims=True) + jnp.sum(new_exp, -1, keepdims=True)
        old_weights = (old_exp / totals).astype(jnp.bfloat16)
        new_weights = (new_exp / totals).astype(jnp.bfloat16)
        result = jnp.einsum(
            "btkgc,bckd->btkgd",
            old_weights,
            cached[:, :, :, 1, :],
            preferred_element_type=jnp.float32,
        )
        result = result + jnp.einsum(
            "btkgs,bskd->btkgd",
            new_weights,
            fresh_rows[:, :, :, 1, :],
            preferred_element_type=jnp.float32,
        )
        return result.astype(jnp.bfloat16).reshape(block_rows, 2, local_kv * group_size * HEAD_DIM)

    decoded = lax.map(
        decode_block,
        (
            new_queries.reshape(count_blocks, block_rows, 2, new_queries.shape[2]),
            block_table.reshape(count_blocks, block_rows, block_table.shape[1]),
            lengths.reshape(count_blocks, block_rows),
            fresh.reshape(count_blocks, block_rows, 2, local_kv, 2, HEAD_DIM),
        ),
    )
    decoded = decoded.reshape(row_count, 2, new_queries.shape[2])
    doc_row = documents[0]
    train_places = jnp.arange(train_count, dtype=jnp.int32)
    allowed = (train_places[None, :] <= train_places[:, None]) & (
        doc_row[None, :] == doc_row[:, None]
    )
    heads_train = train_queries.reshape(train_count, local_kv, group_size, HEAD_DIM)
    scores = (
        jnp.einsum(
            "tkgd,skd->kgts", heads_train, train_kv[:, :, 0, :], preferred_element_type=jnp.float32
        )
        * scaling
    )
    scores = jnp.where(allowed[None, None, :, :], scores, masked_value)
    highest = jnp.max(scores, -1, keepdims=True)
    expo = jnp.exp(scores - highest)
    weights = (expo / jnp.sum(expo, -1, keepdims=True)).astype(jnp.bfloat16)
    train_attention = jnp.einsum(
        "kgts,skd->tkgd", weights, train_kv[:, :, 1, :], preferred_element_type=jnp.float32
    )
    train_attention = train_attention.astype(jnp.bfloat16).reshape(
        train_count, train_queries.shape[1]
    )
    return (decoded, train_attention, handover)


def solution(mesh):
    return jax.shard_map(
        local,
        mesh=mesh,
        in_specs=(
            P("fsdp", None, None),
            P("fsdp", None, "tensor"),
            P("fsdp", None, "tensor"),
            P("fsdp", None),
            P("fsdp"),
            P("fsdp"),
            P("fsdp", None),
            P("fsdp", "tensor"),
            P("fsdp", None),
            P("fsdp", "tensor"),
            P("tensor"),
        ),
        out_specs=(P("fsdp", None, "tensor"), P("fsdp", "tensor"), P("fsdp", None, "tensor")),
        check_vma=False,
    )
```

profile of v0, /device:TPU:0, one launch (start us, length us, event | category | flops | bytes accessed | tf_op | source)
XLA Modules:
  0.0 98.4 jit_solution(3456424117043282186)
XLA Ops:
  7.2 0.7 all-gather.2.cloned.1.call-update
  7.9 0.7 compare_and_fusion
  8.7 0.7 compare_select_fusion
  9.7 1.0 %reshape.141 = bf16[16,2,2,8,128]{4,3,2,1,0:T(8,128)(2,1)S(1)} reshape(bf16[16,2,2048]{2,1,0:T(2,128)(2,1)} %param.12) | data formatting | bytes 262144 | tf_op jit(solution)/shard_map/while/body/eval_jaxpr/reshape | solution.py:67
  10.8 1.0 %copy.53 = bf16[8,8,16,128]{3,2,1,0:T(8,128)(2,1)S(1)} copy(bf16[8,8,16,128]{3,1,2,0:T(8,128)(2,1)} %bitcast.89) | data formatting | bytes 524288
  11.8 1.2 %reshape.142 = bf16[32,8192]{1,0:T(8,128)(2,1)S(1)} reshape(bf16[16,2,8192]{2,1,0:T(2,128)(2,1)} %param.11) | data formatting | bytes 1048576 | tf_op jit(solution)/shard_map/reshape | solution.py:34
  13.1 6.7 %gather_fusion = bf16[128,64,512]{2,1,0:T(8,128)(2,1)} fusion(bf16[32,64,512]{2,1,0:T(8,128)(2,1)S(1)} %copy-done, s32[1024]{0:T(1024)S(1)} %pad_clamp_fusion), kind=kCustom, calls=%fused_computation | custom fusion | bytes 16777728 | tf_op jit(solution)/shard_map/while/body/eval_jaxpr/jit(_take)/gather | solution.py:64
  19.8 12.7 %gather.8 = bf16[16,512,2,2,128]{4,3,2,1,0:T(2,128)(2,1)} reshape(bf16[128,64,512]{2,1,0:T(8,128)(2,1)} %gather_fusion) | data formatting | bytes 16777216 | tf_op jit(solution)/shard_map/while/body/eval_jaxpr/jit(_take)/gather | solution.py:64
  32.7 5.3 %copy_select_fusion = bf16[16,512,2,2,128]{4,1,2,0,3:T(8,128)(2,1)S(1)} fusion(bf16[16,512,2,2,128]{4,3,2,1,0:T(2,128)(2,1)} %gather.8, pred[16,512]{1,0:T(8,128)(4,1)S(1)} %broadcast_in_dim.95), kind=kLoop, calls=%fused_computation.2 | loop fusion | flops 4194304 | bytes 16785408 | tf_op jit(solution)/shard_map/while/body/eval_jaxpr/jit(_take)/select_n | solution.py:64
  38.0 4.0 %copy-done.1 = bf16[16,512,2,2,128]{4,1,2,0,3:T(8,128)(2,1)} copy-done((bf16[16,512,2,2,128]{4,1,2,0,3:T(8,128)(2,1)}, bf16[16,512,2,2,128]{4,1,2,0,3:T(8,128)(2,1)S(1)}, u32[]{:S(2)}) %copy-start.1) | copy-done | bytes 8388632
  42.0 2.8 %fusion.35 = (f32[16,2,2,8]{3,1,2,0:T(2,128)}, f32[16,2,2,8,512]{4,3,1,2,0:T(8,128)}) fusion(bf16[16,2,2,8,128]{4,3,2,1,0:T(8,128)(2,1)S(1)} %reshape.141, bf16[16,512,2,2,128]{4,1,2,0,3:T(8,128)(2,1)S(1)} %copy_select_fusion, pred[16,512]{1,0:T(8,128)(4,1)S(1)} %iota_compare_fusion.1), kind=kOutput, calls=%fused_computation.61 | convolution fusion | flops 67894784 | bytes 5384192 | tf_op jit(solution)/shard_map/while/body/eval_jaxpr/btkgd,bckd->btkgc/dot_general | solution.py:69
  44.8 22.1 %all-gather.2.cloned.1.call-done = bf16[8192,512]{1,0:T(8,128)(2,1)} async-done(((bf16[1024,512]{1,0:T(8,128)(2,1)}), bf16[8192,512]{1,0:T(8,128)(2,1)}) %all-gather.2.cloned.1.call-update) | async-done | bytes 8388624 | tf_op jit(solution)/shard_map/all_gather | solution.py:35
  66.9 5.3 %fusion.13 = bf16[64,512]{1,0:T(8,128)(2,1)S(1)} fusion(bf16[64,8192]{1,0:T(8,128)(2,1)} %param.17, bf16[8192,512]{1,0:T(8,128)(2,1)} %all-gather.2.cloned.1.call-done, f32[512]{0:T(512)S(1)} %copy-done.5), kind=kOutput, calls=%fused_computation.21 | convolution fusion | flops 536936448 | bytes 9504768 | tf_op jit(solution)/shard_map/dot_general | solution.py:37
  72.3 1.0 %fusion.37 = f32[2,8,64]{2,1,0:T(8,128)} fusion(bf16[64,2,8,128]{3,2,1,0:T(8,128)(2,1)S(1)} %bitcast.86, pred[64,64]{0,1:T(8,128)(4,1)S(1)} %fusion.26, bf16[64,2,1,128]{3,2,1,0:T(2,128)(2,1)S(1)} %get-tuple-element.25), kind=kOutput, calls=%fused_computation.63 | convolution fusion | flops 17039424 | bytes 303104 | tf_op jit(solution)/shard_map/sub | solution.py:135
  73.3 0.4 fusion.9
  73.7 4.9 %fusion.16 = bf16[32,512]{1,0:T(8,128)(2,1)S(1)} fusion(bf16[32,8192]{1,0:T(8,128)(2,1)S(1)} %reshape.142, bf16[8192,512]{1,0:T(8,128)(2,1)} %all-gather.2.cloned.1.call-done, f32[512]{0:T(512)S(1)} %copy-done.5), kind=kOutput, calls=%fused_computation.26 | convolution fusion | flops 268468224 | bytes 8947712 | tf_op jit(solution)/shard_map/dot_general | solution.py:36
  78.9 0.6 copy.38
  79.5 3.3 %all-to-all-start = ((bf16[8,2,512]{2,1,0:T(2,128)(2,1)}), bf16[8,2,512]{2,1,0:T(2,128)(2,1)S(1)}, u32[]{:S(2)}, u32[]{:S(2)}) async-start(bf16[8,2,512]{2,1,0:T(2,128)(2,1)} %copy.38), calls=%async_computation | async-start | bytes 32768 | tf_op jit(solution)/shard_map/all_to_all | solution.py:54
  82.9 0.7 fusion.36
  83.8 1.6 %fusion.17 = f32[16,2,2,8]{3,1,2,0:T(2,128)S(1)} fusion(f32[16,2,2,8,512]{4,3,1,2,0:T(8,128)} %get-tuple-element.38, f32[16,2,2,8]{3,1,2,0:T(2,128)S(1)} %max.9), kind=kLoop, calls=%fused_computation.30 | loop fusion | flops 523776 | bytes 1052672 | tf_op jit(solution)/shard_map/while/body/eval_jaxpr/reduce_sum | solution.py:94
  85.4 3.2 %fusion.2 = f32[16,2,128,2,8]{2,4,3,1,0:T(8,128)S(1)} fusion(bf16[16,512,2,2,128]{4,1,2,0,3:T(8,128)(2,1)} %copy-done.1, f32[16,2,2,8,512]{4,3,1,2,0:T(8,128)} %get-tuple-element.38, f32[16,2,2,8]{3,1,2,0:T(2,128)S(1)} %add.46, f32[16,2,2,8]{3,1,2,0:T(2,128)S(1)} %max.9), kind=kOutput, calls=%fused_computation.6 | convolution fusion | flops 67895296 | bytes 5509120 | tf_op jit(solution)/shard_map/while/body/eval_jaxpr/btkgc,bckd->btkgd/dot_general | solution.py:97
  89.4 0.8 copy.85
  90.2 0.7 reshape.165
  90.9 0.6 copy.87
  (43 shorter events, 2.0 us)
Async XLA Ops:
  7.2 5.9 %copy-start = (bf16[32,64,512]{2,1,0:T(8,128)(2,1)S(1)}, bf16[32,64,512]{2,1,0:T(8,128)(2,1)}, u32[]{:S(2)}) copy-start(bf16[32,64,512]{2,1,0:T(8,128)(2,1)} %param.13) | copy-start | bytes 6291460
  7.2 59.7 %all-gather.2.cloned.1.call-start = ((), (), s32[]{:S(2)}) async-start(), calls=%async_computation.1 | async-start | bytes 9437184 | tf_op jit(solution)/shard_map/all_gather | solution.py:35
  10.7 27.3 %copy-start.2 = (bf16[16,2,2,8,128]{4,3,2,1,0:T(8,128)(2,1)}, bf16[16,2,2,8,128]{4,3,2,1,0:T(8,128)(2,1)S(1)}, u32[]{:S(2)}) copy-start(bf16[16,2,2,8,128]{4,3,2,1,0:T(8,128)(2,1)S(1)} %reshape.141) | copy-start | bytes 393220
  19.8 12.7 %copy-start.8 = (s32[16]{0:T(128)S(1)}, s32[16]{0:T(128)}, u32[]{:S(2)}) copy-start(s32[16]{0:T(128)} %param.15) | copy-start | bytes 196
  19.8 12.8 %copy-start.6 = (s32[1,64]{1,0:T(1,128)S(1)}, s32[1,64]{1,0:T(1,128)}, u32[]{:S(2)}) copy-start(s32[1,64]{1,0:T(1,128)} %param.19) | copy-start | bytes 772
  32.7 34.2 %copy-start.5 = (f32[512]{0:T(512)S(1)}, f32[512]{0:T(512)}, u32[]{:S(2)}) copy-start(f32[512]{0:T(512)} %param.21) | copy-start | bytes 6148
  38.0 4.0 %copy-start.1 = (bf16[16,512,2,2,128]{4,1,2,0,3:T(8,128)(2,1)}, bf16[16,512,2,2,128]{4,1,2,0,3:T(8,128)(2,1)S(1)}, u32[]{:S(2)}) copy-start(bf16[16,512,2,2,128]{4,1,2,0,3:T(8,128)(2,1)S(1)} %copy_select_fusion) | copy-start | bytes 25165828
  73.7 5.0 %copy-start.7 = (s32[16]{0:T(128)S(1)}, s32[16]{0:T(128)}, u32[]{:S(2)}) copy-start(s32[16]{0:T(128)} %param.16) | copy-start | bytes 196
  73.7 9.2 %copy-start.3 = (bf16[16,2,2,8,128]{4,3,2,1,0:T(8,128)(2,1)S(1)}, bf16[16,2,2,8,128]{4,3,2,1,0:T(8,128)(2,1)}, u32[]{:S(2)}) copy-start(bf16[16,2,2,8,128]{4,3,2,1,0:T(8,128)(2,1)} %copy-done.2) | copy-start | bytes 393220
  73.7 9.9 %copy-start.4 = (f32[16,2,2,8]{3,1,2,0:T(2,128)S(1)}, f32[16,2,2,8]{3,1,2,0:T(2,128)}, u32[]{:S(2)}) copy-start(f32[16,2,2,8]{3,1,2,0:T(2,128)} %get-tuple-element.37) | copy-start | bytes 6148
  78.7 10.2 %copy-start.9 = (f32[2,8,64]{2,1,0:T(8,128)S(1)}, f32[2,8,64]{2,1,0:T(8,128)}, u32[]{:S(2)}) copy-start(f32[2,8,64]{2,1,0:T(8,128)} %fusion.37) | copy-start | bytes 12292
  79.5 11.4 %all-to-all-start = ((bf16[8,2,512]{2,1,0:T(2,128)(2,1)}), bf16[8,2,512]{2,1,0:T(2,128)(2,1)S(1)}, u32[]{:S(2)}, u32[]{:S(2)}) async-start(bf16[8,2,512]{2,1,0:T(2,128)(2,1)} %copy.38), calls=%async_computation | async-start | bytes 32768 | tf_op jit(solution)/shard_map/all_to_all | solution.py:54
Sparse Core Ops, SparseCore 0:
  9.9 56.9 all-gather.1
where the time goes:
time: 99.1 us; the launch traced here: 98.4 us
  local copies, waits for them, and re-layouts  30.2 us (30%)
  waiting for transfers between devices  22.7 us (23%)
  matrix products  19.1 us (19%)
  between operations  14.3 us (14%)
  other arithmetic  8.63 us (9%)
  starting transfers between devices  3.37 us (3%)
    all_gather x1, waiting for transfers between devices, local(): gathered = lax.all_gather(project_weight, 'fsdp', axis=0, tiled=True)  22.1 us
    gather x2, local copies, waits for them, and re-layouts, decode_block(): jnp.take(paged_cache, tables, axis=0)  19.4 us
    unnamed x25, local copies, waits for them, and re-layouts  7.15 us
    select_n x2, other arithmetic, decode_block(): jnp.take(paged_cache, tables, axis=0)  6.03 us
    dot_general x1, matrix products, local(): jnp.dot(train_hidden, gathered, preferred_element_type=jnp.float32)  5.27 us
    dot_general x1, matrix products, local(): decode_sum = jnp.dot(flat_new, gathered, preferred_element_type=jnp.float32)  4.94 us
    all_to_all x1, starting transfers between devices, local(): lax.all_to_all(outgoing, 'fsdp', split_axis=0, concat_axis=0, tiled=True)  3.34 us
    dot_general x1, matrix products, decode_block(): jnp.einsum('btkgc,bckd->btkgd', old_weights, cached[:, :, :, 1, :], prefe...  3.22 us
  transfers between devices with their start and end apart: 2, of which 1 were waited for; matrix products, arithmetic and copies ran while one was open for 41% of the time, Pallas kernels for 0%

commit v1 on v0

v1 whole, which is shorter than its diff:
```python
import functools

import jax
import jax.numpy as jnp
from jax import lax
from jax.experimental import pallas as pl
from jax.experimental.pallas import tpu as pltpu
from jax.sharding import PartitionSpec as P


HEADS = 64
KV_HEADS = 8
HEAD_DIM = 128
GROUP = HEADS // KV_HEADS
SCALING = HEAD_DIM ** (-0.5)
MASKED = -1e30

VMEM_SPEC = pl.BlockSpec(memory_space=pltpu.VMEM)
HBM_SPEC = pl.BlockSpec(memory_space=pltpu.HBM)


def place():
    me = lax.axis_index("fsdp")
    return me % 2, me // 2


def half():
    return lax.axis_index("tensor") % 2


def column_of(row, count, repeat=1):
    shape = (count, row.shape[1])
    picked = lax.broadcasted_iota(jnp.int32, shape, 0) // repeat == lax.broadcasted_iota(
        jnp.int32, shape, 1
    )
    return jnp.sum(jnp.where(picked, row, 0), axis=1, keepdims=True)


def nt_dot(a, b):
    return lax.dot_general(a, b, (((1,), (1,)), ((), ())), preferred_element_type=jnp.float32)


def stacked(ref, head):
    lanes = [(head * GROUP + part) * HEAD_DIM for part in range(GROUP)]
    return jnp.concatenate(
        [ref[..., lane : lane + HEAD_DIM].reshape(-1, HEAD_DIM) for lane in lanes], axis=0
    )


def cached_kernel(
    page, q_hbm, cache_hbm, table_hbm, length_hbm, q_ref, acc_ref, top_ref, total_ref,
    cache_ref, table_ref, length_ref, count_ref, score_ref, sems,
):
    pairs = (
        (table_hbm, table_ref), (length_hbm, length_ref), (q_hbm, q_ref), (cache_hbm, cache_ref)
    )
    copies = [
        pltpu.make_async_copy(source, target, sems.at[index])
        for index, (source, target) in enumerate(pairs)
    ]
    for copy in copies:
        copy.start()
    for copy in copies[:2]:
        copy.wait()
    tokens, columns = cache_ref.shape
    queries = q_ref.shape[0] * 2
    local_kv = columns // (2 * HEAD_DIM)
    chunk = 256
    lane = lax.broadcasted_iota(jnp.int32, (queries, tokens), 1)
    own_page = lane // page
    offset = lane - own_page * page
    length = column_of(length_ref[...], queries, 2)
    count = jnp.zeros((queries, tokens), jnp.float32)
    for block in range(table_ref.shape[0]):
        held = (column_of(table_ref[block : block + 1, :], queries, 2) == own_page) & (
            offset < length - block * page
        )
        count = count + held.astype(jnp.float32)
    count_ref[...] = count
    for copy in copies[2:]:
        copy.wait()

    def times(start):
        return jnp.concatenate([count_ref[:, start : start + chunk]] * GROUP, axis=0)

    for head in range(local_kv):
        base = head * 2 * HEAD_DIM
        q = stacked(q_ref, head)
        top = None
        for start in range(0, tokens, chunk):
            keys = cache_ref[start : start + chunk, base : base + HEAD_DIM]
            scores = jnp.where(times(start) > 0.0, nt_dot(q, keys) * SCALING, MASKED)
            score_ref[:, start : start + chunk] = scores
            top = scores if top is None else jnp.maximum(top, scores)
        top = jnp.max(top, axis=-1, keepdims=True)
        total = jnp.zeros((GROUP * queries, chunk), jnp.float32)
        acc = jnp.zeros((GROUP * queries, HEAD_DIM), jnp.float32)
        for start in range(0, tokens, chunk):
            weights = jnp.exp(score_ref[:, start : start + chunk] - top) * times(start)
            total = total + weights
            acc = acc + jnp.dot(
                weights.astype(jnp.bfloat16),
                cache_ref[start : start + chunk, base + HEAD_DIM : base + 2 * HEAD_DIM],
                preferred_element_type=jnp.float32,
            )
        acc_ref[head] = acc
        top_ref[head] = jnp.broadcast_to(top, acc.shape)
        total_ref[head] = jnp.broadcast_to(jnp.sum(total, axis=-1, keepdims=True), acc.shape)


def slab_kernel(
    new_hbm, train_hbm, target_hbm, bias_hbm, document_hbm, *refs
):
    slabs, (bias_ref, document_ref, target_ref, sems) = refs[:8], refs[8:]
    rows = new_hbm.shape[0]
    width = slabs[0].shape[-1]
    _, chip = place()
    copies = [pltpu.make_async_copy(target_hbm, target_ref, sems.at[0])]
    for index, slab in enumerate(slabs):
        start = pl.multiple_of((chip ^ (index % 4)) * width, 128)
        if index < 4:
            source, slab = new_hbm.at[:, :, pl.ds(start, width)], slab.at[pl.ds(0, rows)]
        else:
            count = slab.shape[0]
            first = half() * count if index == 7 else 0
            source = train_hbm.at[pl.ds(first, count), pl.ds(start, width)]
        copies.append(pltpu.make_async_copy(source, slab, sems.at[1 + index]))
    copies.append(pltpu.make_async_copy(bias_hbm, bias_ref, sems.at[9]))
    copies.append(pltpu.make_async_copy(document_hbm, document_ref, sems.at[10]))
    for copy in copies:
        copy.start()
    copies[0].wait()
    target = target_ref[...].astype(jnp.float32).astype(jnp.bfloat16)
    for slab in slabs[:4]:
        slab[rows, :, :] = jnp.zeros((2, width), jnp.bfloat16)
        slab[rows, :, 0:rows] = jnp.broadcast_to(target, (2, rows))
    for copy in copies[1:]:
        copy.wait()


def halves(total):
    whole = total.astype(jnp.bfloat16)
    rest = (total - whole.astype(jnp.float32)).astype(jnp.bfloat16)
    keys = [
        rest[:, start : start + HEAD_DIM] for start in range(0, total.shape[1], 2 * HEAD_DIM)
    ]
    return jnp.concatenate([whole] + keys, axis=1)


def widened(parts):
    parts = parts.astype(jnp.float32)
    columns = parts.shape[1] * 2 // 3
    pieces = []
    for start in range(0, columns, 2 * HEAD_DIM):
        middle, rest = start + HEAD_DIM, columns + start // 2
        pieces.append(parts[:, start:middle] + parts[:, rest : rest + HEAD_DIM])
        pieces.append(parts[:, middle : middle + HEAD_DIM])
    return jnp.concatenate(pieces, axis=1)


def product(rows, weight_ref, partner_ref):
    depth = weight_ref.shape[0]
    core, _ = place()
    is_first = core == 0
    low, high = rows[:, :depth], rows[:, depth:]
    own = jnp.where(is_first, low, high)
    other = jnp.where(is_first, high, low)
    return jnp.dot(own, weight_ref[...], preferred_element_type=jnp.float32) + jnp.dot(
        other, partner_ref[...], preferred_element_type=jnp.float32
    )


def train_product_kernel(
    weight_ref, partner_ref, bias_ref, own_ref, first_ref, second_ref, near_ref, far_ref, *outs
):
    sources = (own_ref, first_ref, second_ref, near_ref, far_ref)
    count = own_ref.shape[0]
    total = product(
        jnp.concatenate([ref[...] for ref in sources], axis=0), weight_ref, partner_ref
    )
    outs[0][...] = total[:count] + bias_ref[...]
    outs[1][...] = halves(total[count : 2 * count])
    outs[2][...] = halves(total[2 * count : 3 * count])
    part = halves(total[3 * count :])
    near, far = part[: count // 2], part[count // 2 :]
    start = pl.multiple_of(half() * (count // 2), 16)
    outs[3][pl.ds(start, count // 2)] = near
    outs[3][pl.ds(pl.multiple_of(count // 2 - start, 16), count // 2)] = far


def new_product_kernel(weight_ref, partner_ref, bias_ref, *refs):
    sources, outs, kept_ref = refs[:4], refs[4:8], refs[8]
    rows = sources[0].shape[0] - 1
    count = 2 * rows
    slabs = [ref[:rows].reshape(count, ref.shape[-1]) for ref in sources]
    total = product(jnp.concatenate(slabs, axis=0), weight_ref, partner_ref)
    parts = [total[index * count : (index + 1) * count] for index in range(4)]
    parts[0] = parts[0] + bias_ref[...]
    outs[0][...] = parts[0]
    parts = [halves(part) for part in parts]
    _, chip = place()
    row = lax.broadcasted_iota(jnp.int32, (64, 1), 0)
    mask, core, seen, token = row // 16, (row // 8) % 2, (row // 2) % 4, row % 2
    shard = (2 * (chip ^ mask) + core).astype(jnp.float32)
    entry = lax.broadcasted_iota(jnp.int32, (rows, count), 0)
    lane = lax.broadcasted_iota(jnp.int32, (rows, count), 1)
    moved = None
    for index, ref in enumerate(sources):
        target = ref[rows, :, 0:rows].astype(jnp.float32)[:1]
        target = column_of(target, rows)
        target = jnp.sum(jnp.where(lane // 2 == entry, target, 0.0), axis=0, keepdims=True)
        chosen = (target == shard) & (token == lane[:1] % 2) & ((mask ^ seen) == index)
        picked = jnp.dot(
            chosen.astype(jnp.bfloat16), parts[index], preferred_element_type=jnp.float32
        )
        moved = picked if moved is None else moved + picked
    kept_ref[...] = widened(moved[:16])
    moved = moved.astype(jnp.bfloat16)
    for index in range(1, 4):
        outs[index][:count] = parts[index]
        outs[index][count:] = moved[16 * index : 16 * (index + 1)]


def pick(target_ref, fresh, shards):
    count, lanes = target_ref.shape[1], fresh.shape[0]
    row = lax.broadcasted_iota(jnp.int32, (count, lanes), 0)
    lane = lax.broadcasted_iota(jnp.int32, (count, lanes), 1)
    column = column_of(target_ref[...], count)
    target = jnp.sum(jnp.where(lane // 2 == row, column, 0), axis=0, keepdims=True)
    token = lax.broadcasted_iota(jnp.int32, (shards.shape[0], lanes), 0) % 2
    lane = lax.broadcasted_iota(jnp.int32, (shards.shape[0], lanes), 1) % 2
    chosen = (target == shards) & (token == lane)
    return jnp.dot(chosen.astype(jnp.bfloat16), fresh, preferred_element_type=jnp.float32)


def fresh_kernel(target_ref, own_ref, fresh_ref, outgoing_ref):
    fresh = own_ref[...].astype(jnp.bfloat16)
    fresh_ref[...] = fresh
    shards = lax.broadcasted_iota(jnp.int32, (2 * outgoing_ref.shape[0], 1), 0) // 2
    outgoing = pick(target_ref, fresh, shards)
    outgoing_ref[...] = outgoing.reshape(outgoing_ref.shape).astype(jnp.bfloat16)


def paired_fresh_kernel(own_ref, kept_ref, *refs):
    sources, (fresh_ref, moved_ref) = refs[:-2], refs[-2:]
    count = own_ref.shape[0]
    fresh, moved = own_ref[...], kept_ref[...]
    for ref in sources:
        arrived = widened(ref[...])
        fresh = fresh + arrived[:count]
        moved = moved + arrived[count:]
    fresh_ref[...] = fresh.astype(jnp.bfloat16)
    moved_ref[...] = moved.astype(jnp.bfloat16)


def decode_kernel(fresh_ref, q_ref, acc_ref, top_ref, total_ref, decoded_ref):
    queries = fresh_ref.shape[0]
    local_kv = fresh_ref.shape[1] // (2 * HEAD_DIM)
    row = lax.broadcasted_iota(jnp.int32, (queries, queries), 0)
    column = lax.broadcasted_iota(jnp.int32, (queries, queries), 1)
    allowed = (row // 2 == column // 2) & (column <= row)
    allowed = jnp.concatenate([allowed.astype(jnp.float32)] * GROUP, axis=0) > 0.0
    for head in range(local_kv):
        base = head * 2 * HEAD_DIM
        middle, end = base + HEAD_DIM, base + 2 * HEAD_DIM
        scores = nt_dot(stacked(q_ref, head), fresh_ref[:, base:middle]) * SCALING
        scores = jnp.where(allowed, scores, MASKED)
        old_top = top_ref[head][:, :1]
        top = jnp.maximum(old_top, jnp.max(scores, axis=-1, keepdims=True))
        shrink = jnp.exp(old_top - top)
        weights = jnp.exp(scores - top)
        total = total_ref[head][:, :1] * shrink + jnp.sum(weights, axis=-1, keepdims=True)
        result = acc_ref[head] * shrink + jnp.dot(
            weights.astype(jnp.bfloat16),
            fresh_ref[:, middle:end],
            preferred_element_type=jnp.float32,
        )
        result = result / total
        for part in range(GROUP):
            lane = (head * GROUP + part) * HEAD_DIM
            decoded_ref[:, :, lane : lane + HEAD_DIM] = (
                result[part * queries : (part + 1) * queries]
                .reshape(queries // 2, 2, HEAD_DIM)
                .astype(jnp.bfloat16)
            )


def paired_train_kernel(
    q_ref, document_ref, same_ref, other_ref, own_ref, *refs
):
    sources, (train_ref, handover_ref) = refs[:-2], refs[-2:]
    core, chip = place()
    for source, ref in ((core, same_ref), (1 - core, other_ref)):
        rows = ref[...].astype(jnp.float32)
        rows = jnp.where(core == 0, rows[:8], rows[8:])
        for mask in range(4):
            pair = rows[2 * mask : 2 * mask + 2].astype(jnp.bfloat16)
            handover_ref[2 * (chip ^ mask) + source] = pair
    total = own_ref[...]
    for ref in sources:
        total = total + widened(ref[...])
    train_attend(q_ref, document_ref, total.astype(jnp.bfloat16), train_ref)


def train_kernel(q_ref, document_ref, own_ref, train_ref):
    train_attend(q_ref, document_ref, own_ref[...].astype(jnp.bfloat16), train_ref)


def train_attend(q_ref, document_ref, keys_values, train_ref):
    tokens = q_ref.shape[0]
    local_kv = keys_values.shape[1] // (2 * HEAD_DIM)
    row = lax.broadcasted_iota(jnp.int32, (tokens, tokens), 0)
    column = lax.broadcasted_iota(jnp.int32, (tokens, tokens), 1)
    allowed = (column <= row) & (
        document_ref[...] == column_of(document_ref[...], tokens)
    )
    allowed = jnp.concatenate([allowed.astype(jnp.float32)] * GROUP, axis=0) > 0.0
    for head in range(local_kv):
        base = head * 2 * HEAD_DIM
        middle, end = base + HEAD_DIM, base + 2 * HEAD_DIM
        scores = nt_dot(stacked(q_ref, head), keys_values[:, base:middle]) * SCALING
        scores = jnp.where(allowed, scores, MASKED)
        weights = jnp.exp(scores - jnp.max(scores, axis=-1, keepdims=True))
        total = jnp.sum(weights, axis=-1, keepdims=True)
        result = jnp.dot(
            weights.astype(jnp.bfloat16),
            keys_values[:, middle:end],
            preferred_element_type=jnp.float32,
        )
        result = (result / total).astype(jnp.bfloat16)
        for part in range(GROUP):
            lane = (head * GROUP + part) * HEAD_DIM
            train_ref[:, lane : lane + HEAD_DIM] = result[part * tokens : (part + 1) * tokens]


def exchange(parts, core_groups):
    return lax.all_to_all(
        parts, "fsdp", split_axis=0, concat_axis=0, tiled=True, axis_index_groups=core_groups
    )


def call(kernel, outs, *operands, in_place=0, room=12, **options):
    single = not isinstance(outs, tuple)
    left = len(operands) - in_place
    return pl.pallas_call(
        kernel,
        out_shape=outs,
        in_specs=[HBM_SPEC] * in_place + [VMEM_SPEC] * left,
        out_specs=VMEM_SPEC if single else (VMEM_SPEC,) * len(outs),
        compiler_params=pltpu.CompilerParams(vmem_limit_bytes=room << 20),
        **options,
    )(
        *[pltpu.with_memory_space_constraint(value, pltpu.HBM) for value in operands[:in_place]],
        *operands[in_place:],
    )


def steps(
    new_hidden,
    new_queries,
    paged_cache,
    block_table,
    lengths,
    destination,
    train_hidden,
    train_queries,
    documents,
    project_weight,
    project_bias,
):
    row_count = new_hidden.shape[0]
    depth, columns = project_weight.shape
    local_kv = columns // (2 * HEAD_DIM)
    train_count = train_hidden.shape[0]
    size = lax.axis_size("fsdp")

    def swap(value):
        return lax.ppermute(value, "fsdp", [(i, i ^ 1) for i in range(size)])

    chips = size // 2
    fresh_count = row_count * 2

    def shape(dims, dtype=jnp.bfloat16):
        return jax.ShapeDtypeStruct(dims, dtype)

    pool, page, _ = paged_cache.shape
    stack = GROUP * fresh_count
    state = shape((local_kv, stack, HEAD_DIM), jnp.float32)
    tokens = pool * page
    cached_inputs = (
        new_queries,
        paged_cache.reshape(tokens, columns),
        block_table.T,
        lengths[None, :],
    )
    staged, acc, top, totals = call(
        functools.partial(cached_kernel, page),
        (shape(new_queries.shape), state, state, state),
        *cached_inputs,
        in_place=4,
        scratch_shapes=[
            pltpu.VMEM((tokens, columns), jnp.bfloat16),
            pltpu.VMEM(block_table.shape[::-1], jnp.int32),
            pltpu.VMEM((1, row_count), jnp.int32),
            pltpu.VMEM((fresh_count, tokens), jnp.float32),
            pltpu.VMEM((stack, tokens), jnp.float32),
            pltpu.SemaphoreType.DMA((4,)),
        ],
        room=24,
    )
    partner_weight = swap(project_weight)
    fresh_type = shape((fresh_count, columns))
    outgoing_type = shape((size, 2, columns))
    decode_state = (staged, acc, top, totals)
    train_inputs = (train_queries, documents)
    decoded_type, train_type = shape(new_queries.shape), shape(train_queries.shape)

    beside = lax.axis_size("tensor")
    if chips == 4 and beside % 2 == 0 and train_count % 32 == 0:
        def hop(value, mask):
            return lax.ppermute(value, "fsdp", [(i, i ^ (2 * mask)) for i in range(size)])

        wide = columns * 3 // 2

        def products(kernel, sources, rows, extra):
            outs = [shape((rows, columns), jnp.float32)] + [shape((rows + extra, wide))] * 3
            if extra:
                outs.append(shape((extra, columns), jnp.float32))
            return call(kernel, tuple(outs), project_weight, partner_weight, bias, *sources)

        others = (1, 2, 3)
        *slabs, bias, pack = call(
            slab_kernel,
            (shape((row_count + 1, 2, 2 * depth)),) * 4
            + (shape((train_count, 2 * depth)),) * 3
            + (shape((train_count // 2, 2 * depth)),)
            + (shape((1, columns), jnp.float32), shape(documents.shape, jnp.int32)),
            new_hidden,
            train_hidden,
            destination[None, :],
            project_bias[None, :],
            documents,
            in_place=5,
            scratch_shapes=[
                pltpu.VMEM((1, row_count), jnp.int32),
                pltpu.SemaphoreType.DMA((11,)),
            ],
        )
        new_slabs, train_slabs = slabs[:4], slabs[4:]
        new_rows = [hop(new_slabs[mask], mask) for mask in others]
        train_rows = [hop(train_slabs[mask], mask) for mask in others]
        own, first, second, third, kept = products(
            new_product_kernel, [new_slabs[0]] + new_rows, fresh_count, 16
        )
        back = [hop(part, mask) for mask, part in zip(others, (first, second, third))]
        fresh, same = call(
            paired_fresh_kernel, (fresh_type, shape((16, columns))), own, kept, *back
        )
        other = swap(same)
        far = lax.ppermute(train_rows[2], "tensor", [(i, i ^ 1) for i in range(beside)])
        train_own, first, second, third = products(
            train_product_kernel, [train_slabs[0]] + train_rows + [far], train_count, 0
        )
        train_back = [hop(part, mask) for mask, part in zip(others, (first, second, third))]
        decoded = call(decode_kernel, decoded_type, fresh, *decode_state)
        train_attention, handover = call(
            paired_train_kernel,
            (train_type, outgoing_type),
            train_queries,
            pack,
            same,
            other,
            train_own,
            *train_back,
        )
        return (decoded, train_attention, handover)

    def gathered(hidden):
        rows = hidden.reshape(-1, chips, 2 * depth)
        count = rows.shape[0]
        arrived = exchange(rows.transpose(1, 0, 2), groups)
        partial = jnp.dot(
            arrived.reshape(chips * count, 2 * depth),
            weight,
            preferred_element_type=jnp.float32,
        )
        partial = partial.astype(jnp.bfloat16).reshape(chips, count, columns)
        parts = exchange(partial, groups)
        return jnp.sum(parts.astype(jnp.float32), axis=0) + project_bias

    core = lax.axis_index("fsdp") % 2
    weight = jnp.where(
        core == 0,
        jnp.concatenate([project_weight, partner_weight], axis=0),
        jnp.concatenate([partner_weight, project_weight], axis=0),
    )
    groups = [[2 * c + k for c in range(chips)] for k in range(2)]
    fresh, outgoing = call(
        fresh_kernel, (fresh_type, outgoing_type), destination[None, :], gathered(new_hidden)
    )
    handover = lax.all_to_all(outgoing, "fsdp", split_axis=0, concat_axis=0, tiled=True)
    decoded = call(decode_kernel, decoded_type, fresh, *decode_state)
    train_attention = call(train_kernel, train_type, *train_inputs, gathered(train_hidden))
    return (decoded, train_attention, handover)


def solution(mesh):
    return jax.shard_map(
        steps,
        mesh=mesh,
        in_specs=(
            P("fsdp", None, None),
            P("fsdp", None, "tensor"),
            P("fsdp", None, "tensor"),
            P("fsdp", None),
            P("fsdp"),
            P("fsdp"),
            P("fsdp", None),
            P("fsdp", "tensor"),
            P("fsdp", None),
            P("fsdp", "tensor"),
            P("tensor"),
        ),
        out_specs=(P("fsdp", None, "tensor"), P("fsdp", "tensor"), P("fsdp", None, "tensor")),
        check_vma=False,
    )
```

time: 99.1 us -> 42.8 us (0.43)
  local copies, waits for them, and re-layouts: 30.2 us -> 0.01 us
  matrix products: 19.1 us -> 0 us
  starting transfers between devices: 3.37 us -> 18.9 us
  between operations: 14.3 us -> 0.72 us
  Pallas kernels: 0 us -> 9.83 us
  waiting for transfers between devices: 22.7 us -> 13.2 us
  other arithmetic: 8.63 us -> 0 us
    all_gather x1 -> x0, waiting for transfers between devices: 22.1 us -> none  [local(): gathered = lax.all_gather(project_weight, 'fsdp', axis=0, tiled=True)]
    gather x2 -> x0, local copies, waits for them, and re-layouts: 19.4 us -> none  [decode_block(): jnp.take(paged_cache, tables, axis=0)]
    ppermute x0 -> x15, starting transfers between devices: none -> 18.9 us  [the longest x12 16.6 us: hop(): return lax.ppermute(value, 'fsdp', [(i, i ^ 2 * mask) for i in range(size)])]
    dot_general x9 -> x0, matrix products: 18.1 us -> none  [the longest x1 5.27 us: local(): jnp.dot(train_hidden, gathered, preferred_element_type=jnp.float32)]
    ppermute x0 -> x15, waiting for transfers between devices: none -> 13.2 us  [the longest x12 13.1 us: hop(): return lax.ppermute(value, 'fsdp', [(i, i ^ 2 * mask) for i in range(size)])]
    pallas_call x0 -> x7, Pallas kernels: none -> 9.83 us  [call(): pl.pallas_call(kernel, out_shape=outs, in_specs=[HBM_SPEC] * in_place + [...]
    unnamed x25 -> x4, local copies, waits for them, and re-layouts: 7.15 us -> 0.01 us
    select_n x2 -> x0, other arithmetic: 6.03 us -> none  [decode_block(): jnp.take(paged_cache, tables, axis=0)]
  transfers between devices with their start and end apart: 2 -> 15, of which waited for: 1 -> 5; matrix products, arithmetic and copies ran while one was open for 41% -> 0% of each run, Pallas kernels for 0% -> 20%
where the time goes in v1:
time: 42.8 us; the launch traced here: 42.6 us
  starting transfers between devices  18.9 us (44%)
  waiting for transfers between devices  13.2 us (31%)
  Pallas kernels  9.83 us (23%)
  between operations  0.72 us (2%)
    ppermute x12, starting transfers between devices, hop(): return lax.ppermute(value, 'fsdp', [(i, i ^ 2 * mask) for i in range(size)])  16.6 us
    ppermute x12, waiting for transfers between devices, hop(): return lax.ppermute(value, 'fsdp', [(i, i ^ 2 * mask) for i in range(size)])  13.1 us
    pallas_call x7, Pallas kernels, call(): pl.pallas_call(kernel, out_shape=outs, in_specs=[HBM_SPEC] * in_place + [...  9.83 us
    ppermute x1, starting transfers between devices, steps(): lax.ppermute(train_rows[2], 'tensor', [(i, i ^ 1) for i in range(beside)])  1.58 us
  transfers between devices with their start and end apart: 15, of which 5 were waited for; matrix products, arithmetic and copies ran while one was open for 0% of the time, Pallas kernels for 20%

profile of v1, /device:TPU:0, one launch (start us, length us, event | category | flops | bytes accessed | tf_op | source)
XLA Modules:
  0.0 42.6 jit_solution(13304449205576025797)
XLA Ops:
  0.6 0.6 %collective-permute-start = (bf16[1024,512]{1,0:T(8,128)(2,1)}, bf16[1024,512]{1,0:T(8,128)(2,1)S(1)}, u32[]{:S(2)}, u32[]{:S(2)}) collective-permute-start(bf16[1024,512]{1,0:T(8,128)(2,1)} %weight_ref.3), channel_id=1, source_target_pairs={{0,4},{4,0},{8,12},{12,8},{16,20},{20,16},{24,28},{28,24},{1,5},{5... | collective-permute-start | bytes 3145736 | tf_op jit(solution)/shard_map/ppermute | solution.py:378
  1.2 1.5 %shard_map.130 = (bf16[17,2,2048]{2,1,0:T(2,128)(2,1)S(1)}, bf16[17,2,2048]{2,1,0:T(2,128)(2,1)S(1)}, bf16[17,2,2048]{2,1,0:T(2,128)(2,1)S(1)}, bf16[17,2,2048]{...) custom-call(bf16[16,2,8192]{2,1,0:T(2,128)(2,1)} %new_hbm.1, ...), custom_call_target="tpu_custom_call" | custom-call | tf_op jit(solution)/shard_map/pallas_call | solution.py:345
  2.7 3.6 %collective-permute-start.10 = (bf16[32,2048]{1,0:T(8,128)(2,1)S(1)}, bf16[32,2048]{1,0:T(8,128)(2,1)S(1)}, u32[]{:S(2)}, u32[]{:S(2)}) collective-permute-start(bf16[32,2048]{1,0:T(8,128)(2,1)S(1)} %get-tuple-element.50), channel_id=1, source_target_pairs={{0,24},{4,28},{8,16},{12,20},{16,8},{20,12},{24,0},{28,4},{1,25},{... | collective-permute-start | bytes 393224 | tf_op jit(solution)/shard_map/ppermute | solution.py:421
  6.3 0.5 %collective-permute-start.1 = (bf16[17,2,2048]{2,1,0:T(2,128)(2,1)S(1)}, bf16[17,2,2048]{2,1,0:T(2,128)(2,1)S(1)}, u32[]{:S(2)}, u32[]{:S(2)}) collective-permute-start(bf16[17,2,2048]{2,1,0:T(2,128)(2,1)S(1)} %get-tuple-element.32), channel_id=1, source_target_pairs={{0,8},{4,12},{8,0},{12,4},{16,24},{20,28},{24,16},{28,20},{1,9},{5... | collective-permute-start | bytes 417800 | tf_op jit(solution)/shard_map/ppermute | solution.py:421
  7.0 1.9 %collective-permute-start.8 = (bf16[64,2048]{1,0:T(8,128)(2,1)S(1)}, bf16[64,2048]{1,0:T(8,128)(2,1)S(1)}, u32[]{:S(2)}, u32[]{:S(2)}) collective-permute-start(bf16[64,2048]{1,0:T(8,128)(2,1)S(1)} %get-tuple-element.48), channel_id=1, source_target_pairs={{0,8},{4,12},{8,0},{12,4},{16,24},{20,28},{24,16},{28,20},{1,9},{5... | collective-permute-start | bytes 786440 | tf_op jit(solution)/shard_map/ppermute | solution.py:421
  8.8 1.8 %collective-permute-done.10.near_ref = bf16[32,2048]{1,0:T(8,128)(2,1)S(1)} collective-permute-done((bf16[32,2048]{1,0:T(8,128)(2,1)S(1)}, bf16[32,2048]{1,0:T(8,128)(2,1)S(1)}, u32[]{:S(2)}, u32[]{:S(2)}) %collective-permute-start.10) | collective-permute-done | bytes 131104 | tf_op jit(solution)/shard_map/ppermute | solution.py:421
  10.7 2.0 %collective-permute-start.9 = (bf16[64,2048]{1,0:T(8,128)(2,1)S(1)}, bf16[64,2048]{1,0:T(8,128)(2,1)S(1)}, u32[]{:S(2)}, u32[]{:S(2)}) collective-permute-start(bf16[64,2048]{1,0:T(8,128)(2,1)S(1)} %get-tuple-element.49), channel_id=1, source_target_pairs={{0,16},{4,20},{8,24},{12,28},{16,0},{20,4},{24,8},{28,12},{1,17},{... | collective-permute-start | bytes 786440 | tf_op jit(solution)/shard_map/ppermute | solution.py:421
  12.7 1.5 %collective-permute-done.1.refs_1_ = bf16[17,2,2048]{2,1,0:T(2,128)(2,1)S(1)} collective-permute-done((bf16[17,2,2048]{2,1,0:T(2,128)(2,1)S(1)}, bf16[17,2,2048]{2,1,0:T(2,128)(2,1)S(1)}, u32[]{:S(2)}, u32[]{:S(2)}) %collective-permute-start.1) | collective-permute-done | bytes 139296 | tf_op jit(solution)/shard_map/ppermute | solution.py:421
  14.2 1.4 %collective-permute-start.3 = (bf16[17,2,2048]{2,1,0:T(2,128)(2,1)S(1)}, bf16[17,2,2048]{2,1,0:T(2,128)(2,1)S(1)}, u32[]{:S(2)}, u32[]{:S(2)}) collective-permute-start(bf16[17,2,2048]{2,1,0:T(2,128)(2,1)S(1)} %get-tuple-element.34), channel_id=1, source_target_pairs={{0,24},{4,28},{8,16},{12,20},{16,8},{20,12},{24,0},{28,4},{1,25},{... | collective-permute-start | bytes 417800 | tf_op jit(solution)/shard_map/ppermute | solution.py:421
  15.6 1.6 %collective-permute-start.11 = (bf16[32,2048]{1,0:T(8,128)(2,1)S(1)}, bf16[32,2048]{1,0:T(8,128)(2,1)S(1)}, u32[]{:S(2)}, u32[]{:S(2)}) collective-permute-start(bf16[32,2048]{1,0:T(8,128)(2,1)S(1)} %collective-permute-done.10.near_ref), channel_id=1, source_target_pairs={{0,1},{1,0},{2,3},{3,2},{4,5},{5,4},{6,7},{7,6},{8,9},{9,8},{10,11... | collective-permute-start | bytes 393224 | tf_op jit(solution)/shard_map/ppermute | solution.py:460
  17.2 4.8 %collective-permute-done.3.refs_3_ = bf16[17,2,2048]{2,1,0:T(2,128)(2,1)S(1)} collective-permute-done((bf16[17,2,2048]{2,1,0:T(2,128)(2,1)S(1)}, bf16[17,2,2048]{2,1,0:T(2,128)(2,1)S(1)}, u32[]{:S(2)}, u32[]{:S(2)}) %collective-permute-start.3) | collective-permute-done | bytes 139296 | tf_op jit(solution)/shard_map/ppermute | solution.py:421
  22.0 0.8 %shard_map.131 = (f32[32,512]{1,0:T(8,128)S(1)}, bf16[48,768]{1,0:T(8,128)(2,1)S(1)}, bf16[48,768]{1,0:T(8,128)(2,1)S(1)}, bf16[48,768]{1,0:T(8,128)(2,1)S(1)}, f32[16,512]{1,0:T(8,128)S(1)}) custom-call(bf16[1024,512]{1,0:T(8,128)(2,1)S(1)} %copy-done, bf16[1024,512]{1,0:T(8,128)(2,1)S(1)} %collective-permute-done.partner_ref, ...), custom_call_target="tpu_custom_call" | custom-call | tf_op jit(solution)/shard_map/pallas_call | solution.py:345
  22.8 1.7 %collective-permute-start.4 = (bf16[48,768]{1,0:T(8,128)(2,1)S(1)}, bf16[48,768]{1,0:T(8,128)(2,1)S(1)}, u32[]{:S(2)}, u32[]{:S(2)}) collective-permute-start(bf16[48,768]{1,0:T(8,128)(2,1)S(1)} %get-tuple-element.37), channel_id=1, source_target_pairs={{0,8},{4,12},{8,0},{12,4},{16,24},{20,28},{24,16},{28,20},{1,9},{5... | collective-permute-start | bytes 221192 | tf_op jit(solution)/shard_map/ppermute | solution.py:421
  24.5 0.7 %shard_map.135 = (f32[64,512]{1,0:T(8,128)S(1)}, bf16[64,768]{1,0:T(8,128)(2,1)S(1)}, bf16[64,768]{1,0:T(8,128)(2,1)S(1)}, bf16[64,768]{1,0:T(8,128)(2,1)S(1)}) custom-call(bf16[1024,512]{1,0:T(8,128)(2,1)S(1)} %copy-done, bf16[1024,512]{1,0:T(8,128)(2,1)S(1)} %collective-permute-done.partner_ref, f32[1,512]{1,0:T(1,128)S(1)} %get-tuple-element.30.bias_ref, ...), custom_call_target="tpu_custom_call" | custom-call | tf_op jit(solution)/shard_map/pallas_call | solution.py:345
  25.3 0.4 collective-permute-start.12
  25.7 1.8 %collective-permute-start.13 = (bf16[64,768]{1,0:T(8,128)(2,1)S(1)}, bf16[64,768]{1,0:T(8,128)(2,1)S(1)}, u32[]{:S(2)}, u32[]{:S(2)}) collective-permute-start(bf16[64,768]{1,0:T(8,128)(2,1)S(1)} %get-tuple-element.53), channel_id=1, source_target_pairs={{0,16},{4,20},{8,24},{12,28},{16,0},{20,4},{24,8},{28,12},{1,17},{... | collective-permute-start | bytes 294920 | tf_op jit(solution)/shard_map/ppermute | solution.py:421
  27.4 1.4 %collective-permute-start.14 = (bf16[64,768]{1,0:T(8,128)(2,1)S(1)}, bf16[64,768]{1,0:T(8,128)(2,1)S(1)}, u32[]{:S(2)}, u32[]{:S(2)}) collective-permute-start(bf16[64,768]{1,0:T(8,128)(2,1)S(1)} %get-tuple-element.54), channel_id=1, source_target_pairs={{0,24},{4,28},{8,16},{12,20},{16,8},{20,12},{24,0},{28,4},{1,25},{... | collective-permute-start | bytes 294920 | tf_op jit(solution)/shard_map/ppermute | solution.py:421
  28.8 1.6 %collective-permute-start.5 = (bf16[48,768]{1,0:T(8,128)(2,1)S(1)}, bf16[48,768]{1,0:T(8,128)(2,1)S(1)}, u32[]{:S(2)}, u32[]{:S(2)}) collective-permute-start(bf16[48,768]{1,0:T(8,128)(2,1)S(1)} %get-tuple-element.38), channel_id=1, source_target_pairs={{0,16},{4,20},{8,24},{12,28},{16,0},{20,4},{24,8},{28,12},{1,17},{... | collective-permute-start | bytes 221192 | tf_op jit(solution)/shard_map/ppermute | solution.py:421
  30.4 0.3 collective-permute-start.6
  30.6 4.1 %collective-permute-done.5.refs_1_ = bf16[48,768]{1,0:T(8,128)(2,1)S(1)} collective-permute-done((bf16[48,768]{1,0:T(8,128)(2,1)S(1)}, bf16[48,768]{1,0:T(8,128)(2,1)S(1)}, u32[]{:S(2)}, u32[]{:S(2)}) %collective-permute-start.5) | collective-permute-done | bytes 73760 | tf_op jit(solution)/shard_map/ppermute | solution.py:421
  34.8 0.9 %collective-permute-done.6.refs_2_ = bf16[48,768]{1,0:T(8,128)(2,1)S(1)} collective-permute-done((bf16[48,768]{1,0:T(8,128)(2,1)S(1)}, bf16[48,768]{1,0:T(8,128)(2,1)S(1)}, u32[]{:S(2)}, u32[]{:S(2)}) %collective-permute-start.6) | collective-permute-done | bytes 73760 | tf_op jit(solution)/shard_map/ppermute | solution.py:421
  35.8 3.9 %shard_map.133 = (bf16[16,2,2048]{2,1,0:T(2,128)(2,1)S(1)}, f32[2,256,128]{2,1,0:T(8,128)S(1)}, f32[2,256,128]{2,1,0:T(8,128)S(1)}, f32[2,256,128]{2,1,0:T(8,128)S(1)}) custom-call(bf16[16,2,2048]{2,1,0:T(2,128)(2,1)} %q_hbm.1, bf16[2048,512]{1,0:T(8,128)(2,1)} %bitcast.5, s32[8,16]{1,0:T(8,128)} %bitcast.6, s32[1,16]{1,0:T(1,128)} %bitcast.9), custom_call_target="tpu_custom_call" | custom-call | tf_op jit(solution)/shard_map/pallas_call | solution.py:345
  39.7 1.5 %shard_map.134 = bf16[16,2,2048]{2,1,0:T(2,128)(2,1)} custom-call(bf16[32,512]{1,0:T(8,128)(2,1)S(1)} %get-tuple-element.40.fresh_ref, bf16[16,2,2048]{2,1,0:T(2,128)(2,1)S(1)} %get-tuple-element.41.q_ref, f32[2,256,128]{2,1,0:T(8,128)S(1)} %get-tuple-element.42.acc_ref, f32[2,256,128]{2,1,0:T(8,128)S(1)} %get-tuple-element.43.top_ref, ...), custom_call_target="tpu_custom_call" | custom-call | tf_op jit(solution)/shard_map/pallas_call | solution.py:345
  41.2 1.4 %shard_map.136 = (bf16[64,2048]{1,0:T(8,128)(2,1)}, bf16[8,2,512]{2,1,0:T(2,128)(2,1)}) custom-call(bf16[64,2048]{1,0:T(8,128)(2,1)S(1)} %copy-done.1, s32[1,64]{1,0:T(1,128)S(1)} %get-tuple-element.45.document_ref, bf16[16,512]{1,0:T(8,128)(2,1)S(1)} %get-tuple-element.46.same_ref, bf16[16,512]{1,0:T(8,128)(2,1)S(1)} %collective-permute-done.7.other_ref, ...), custom_call_target="tpu_custom_call" | custom-call | tf_op jit(solution)/shard_map/pallas_call | solution.py:345
  (17 shorter events, 0.3 us)
Async XLA Ops:
  0.6 21.4 %copy-start = (bf16[1024,512]{1,0:T(8,128)(2,1)S(1)}, bf16[1024,512]{1,0:T(8,128)(2,1)}, u32[]{:S(2)}) copy-start(bf16[1024,512]{1,0:T(8,128)(2,1)} %weight_ref.3) | copy-start | bytes 3145732
  0.6 21.3 %collective-permute-start = (bf16[1024,512]{1,0:T(8,128)(2,1)}, bf16[1024,512]{1,0:T(8,128)(2,1)S(1)}, u32[]{:S(2)}, u32[]{:S(2)}) collective-permute-start(bf16[1024,512]{1,0:T(8,128)(2,1)} %weight_ref.3), channel_id=1, source_target_pairs={{0,4},{4,0},{8,12},{12,8},{16,20},{20,16},{24,28},{28,24},{1,5},{5... | collective-permute-start | bytes 3145736 | tf_op jit(solution)/shard_map/ppermute | solution.py:378
  2.7 7.9 %collective-permute-start.10 = (bf16[32,2048]{1,0:T(8,128)(2,1)S(1)}, bf16[32,2048]{1,0:T(8,128)(2,1)S(1)}, u32[]{:S(2)}, u32[]{:S(2)}) collective-permute-start(bf16[32,2048]{1,0:T(8,128)(2,1)S(1)} %get-tuple-element.50), channel_id=1, source_target_pairs={{0,24},{4,28},{8,16},{12,20},{16,8},{20,12},{24,0},{28,4},{1,25},{... | collective-permute-start | bytes 393224 | tf_op jit(solution)/shard_map/ppermute | solution.py:421
  6.3 7.9 %collective-permute-start.1 = (bf16[17,2,2048]{2,1,0:T(2,128)(2,1)S(1)}, bf16[17,2,2048]{2,1,0:T(2,128)(2,1)S(1)}, u32[]{:S(2)}, u32[]{:S(2)}) collective-permute-start(bf16[17,2,2048]{2,1,0:T(2,128)(2,1)S(1)} %get-tuple-element.32), channel_id=1, source_target_pairs={{0,8},{4,12},{8,0},{12,4},{16,24},{20,28},{24,16},{28,20},{1,9},{5... | collective-permute-start | bytes 417800 | tf_op jit(solution)/shard_map/ppermute | solution.py:421
  6.8 8.8 %collective-permute-start.2 = (bf16[17,2,2048]{2,1,0:T(2,128)(2,1)S(1)}, bf16[17,2,2048]{2,1,0:T(2,128)(2,1)S(1)}, u32[]{:S(2)}, u32[]{:S(2)}) collective-permute-start(bf16[17,2,2048]{2,1,0:T(2,128)(2,1)S(1)} %get-tuple-element.33), channel_id=1, source_target_pairs={{0,16},{4,20},{8,24},{12,28},{16,0},{20,4},{24,8},{28,12},{1,17},{... | collective-permute-start | bytes 417800 | tf_op jit(solution)/shard_map/ppermute | solution.py:421
  7.0 17.6 %collective-permute-start.8 = (bf16[64,2048]{1,0:T(8,128)(2,1)S(1)}, bf16[64,2048]{1,0:T(8,128)(2,1)S(1)}, u32[]{:S(2)}, u32[]{:S(2)}) collective-permute-start(bf16[64,2048]{1,0:T(8,128)(2,1)S(1)} %get-tuple-element.48), channel_id=1, source_target_pairs={{0,8},{4,12},{8,0},{12,4},{16,24},{20,28},{24,16},{28,20},{1,9},{5... | collective-permute-start | bytes 786440 | tf_op jit(solution)/shard_map/ppermute | solution.py:421
  10.7 13.9 %collective-permute-start.9 = (bf16[64,2048]{1,0:T(8,128)(2,1)S(1)}, bf16[64,2048]{1,0:T(8,128)(2,1)S(1)}, u32[]{:S(2)}, u32[]{:S(2)}) collective-permute-start(bf16[64,2048]{1,0:T(8,128)(2,1)S(1)} %get-tuple-element.49), channel_id=1, source_target_pairs={{0,16},{4,20},{8,24},{12,28},{16,0},{20,4},{24,8},{28,12},{1,17},{... | collective-permute-start | bytes 786440 | tf_op jit(solution)/shard_map/ppermute | solution.py:421
  14.2 7.8 %collective-permute-start.3 = (bf16[17,2,2048]{2,1,0:T(2,128)(2,1)S(1)}, bf16[17,2,2048]{2,1,0:T(2,128)(2,1)S(1)}, u32[]{:S(2)}, u32[]{:S(2)}) collective-permute-start(bf16[17,2,2048]{2,1,0:T(2,128)(2,1)S(1)} %get-tuple-element.34), channel_id=1, source_target_pairs={{0,24},{4,28},{8,16},{12,20},{16,8},{20,12},{24,0},{28,4},{1,25},{... | collective-permute-start | bytes 417800 | tf_op jit(solution)/shard_map/ppermute | solution.py:421
  15.6 8.9 %collective-permute-start.11 = (bf16[32,2048]{1,0:T(8,128)(2,1)S(1)}, bf16[32,2048]{1,0:T(8,128)(2,1)S(1)}, u32[]{:S(2)}, u32[]{:S(2)}) collective-permute-start(bf16[32,2048]{1,0:T(8,128)(2,1)S(1)} %collective-permute-done.10.near_ref), channel_id=1, source_target_pairs={{0,1},{1,0},{2,3},{3,2},{4,5},{5,4},{6,7},{7,6},{8,9},{9,8},{10,11... | collective-permute-start | bytes 393224 | tf_op jit(solution)/shard_map/ppermute | solution.py:460
  22.8 7.6 %collective-permute-start.4 = (bf16[48,768]{1,0:T(8,128)(2,1)S(1)}, bf16[48,768]{1,0:T(8,128)(2,1)S(1)}, u32[]{:S(2)}, u32[]{:S(2)}) collective-permute-start(bf16[48,768]{1,0:T(8,128)(2,1)S(1)} %get-tuple-element.37), channel_id=1, source_target_pairs={{0,8},{4,12},{8,0},{12,4},{16,24},{20,28},{24,16},{28,20},{1,9},{5... | collective-permute-start | bytes 221192 | tf_op jit(solution)/shard_map/ppermute | solution.py:421
  25.3 15.9 %copy-start.1 = (bf16[64,2048]{1,0:T(8,128)(2,1)S(1)}, bf16[64,2048]{1,0:T(8,128)(2,1)}, u32[]{:S(2)}) copy-start(bf16[64,2048]{1,0:T(8,128)(2,1)} %q_ref.1) | copy-start | bytes 786436
  25.3 15.9 %collective-permute-start.12 = (bf16[64,768]{1,0:T(8,128)(2,1)S(1)}, bf16[64,768]{1,0:T(8,128)(2,1)S(1)}, u32[]{:S(2)}, u32[]{:S(2)}) collective-permute-start(bf16[64,768]{1,0:T(8,128)(2,1)S(1)} %get-tuple-element.52), channel_id=1, source_target_pairs={{0,8},{4,12},{8,0},{12,4},{16,24},{20,28},{24,16},{28,20},{1,9},{5... | collective-permute-start | bytes 294920 | tf_op jit(solution)/shard_map/ppermute | solution.py:421
  25.7 15.5 %collective-permute-start.13 = (bf16[64,768]{1,0:T(8,128)(2,1)S(1)}, bf16[64,768]{1,0:T(8,128)(2,1)S(1)}, u32[]{:S(2)}, u32[]{:S(2)}) collective-permute-start(bf16[64,768]{1,0:T(8,128)(2,1)S(1)} %get-tuple-element.53), channel_id=1, source_target_pairs={{0,16},{4,20},{8,24},{12,28},{16,0},{20,4},{24,8},{28,12},{1,17},{... | collective-permute-start | bytes 294920 | tf_op jit(solution)/shard_map/ppermute | solution.py:421
  27.4 13.7 %collective-permute-start.14 = (bf16[64,768]{1,0:T(8,128)(2,1)S(1)}, bf16[64,768]{1,0:T(8,128)(2,1)S(1)}, u32[]{:S(2)}, u32[]{:S(2)}) collective-permute-start(bf16[64,768]{1,0:T(8,128)(2,1)S(1)} %get-tuple-element.54), channel_id=1, source_target_pairs={{0,24},{4,28},{8,16},{12,20},{16,8},{20,12},{24,0},{28,4},{1,25},{... | collective-permute-start | bytes 294920 | tf_op jit(solution)/shard_map/ppermute | solution.py:421
  28.8 5.9 %collective-permute-start.5 = (bf16[48,768]{1,0:T(8,128)(2,1)S(1)}, bf16[48,768]{1,0:T(8,128)(2,1)S(1)}, u32[]{:S(2)}, u32[]{:S(2)}) collective-permute-start(bf16[48,768]{1,0:T(8,128)(2,1)S(1)} %get-tuple-element.38), channel_id=1, source_target_pairs={{0,16},{4,20},{8,24},{12,28},{16,0},{20,4},{24,8},{28,12},{1,17},{... | collective-permute-start | bytes 221192 | tf_op jit(solution)/shard_map/ppermute | solution.py:421
  30.4 5.3 %collective-permute-start.6 = (bf16[48,768]{1,0:T(8,128)(2,1)S(1)}, bf16[48,768]{1,0:T(8,128)(2,1)S(1)}, u32[]{:S(2)}, u32[]{:S(2)}) collective-permute-start(bf16[48,768]{1,0:T(8,128)(2,1)S(1)} %get-tuple-element.39), channel_id=1, source_target_pairs={{0,24},{4,28},{8,16},{12,20},{16,8},{20,12},{24,0},{28,4},{1,25},{... | collective-permute-start | bytes 221192 | tf_op jit(solution)/shard_map/ppermute | solution.py:421
  35.7 5.5 %collective-permute-start.7 = (bf16[16,512]{1,0:T(8,128)(2,1)S(1)}, bf16[16,512]{1,0:T(8,128)(2,1)S(1)}, u32[]{:S(2)}, u32[]{:S(2)}) collective-permute-start(bf16[16,512]{1,0:T(8,128)(2,1)S(1)} %get-tuple-element.46.same_ref), channel_id=1, source_target_pairs={{0,4},{4,0},{8,12},{12,8},{16,20},{20,16},{24,28},{28,24},{1,5},{5... | collective-permute-start | bytes 49160 | tf_op jit(solution)/shard_map/ppermute | solution.py:378

commit v2 on v1

--- a/solution.py
+++ b/solution.py
@@ -170,34 +170,32 @@
     )
 
 
-def train_product_kernel(
-    weight_ref, partner_ref, bias_ref, own_ref, first_ref, second_ref, near_ref, far_ref, *outs
-):
-    sources = (own_ref, first_ref, second_ref, near_ref, far_ref)
-    count = own_ref.shape[0]
-    total = product(
-        jnp.concatenate([ref[...] for ref in sources], axis=0), weight_ref, partner_ref
-    )
-    outs[0][...] = total[:count] + bias_ref[...]
-    outs[1][...] = halves(total[count : 2 * count])
-    outs[2][...] = halves(total[2 * count : 3 * count])
-    part = halves(total[3 * count :])
-    near, far = part[: count // 2], part[count // 2 :]
-    start = pl.multiple_of(half() * (count // 2), 16)
-    outs[3][pl.ds(start, count // 2)] = near
-    outs[3][pl.ds(pl.multiple_of(count // 2 - start, 16), count // 2)] = far
-
-
-def new_product_kernel(weight_ref, partner_ref, bias_ref, *refs):
-    sources, outs, kept_ref = refs[:4], refs[4:8], refs[8]
+def second_product_kernel(weight_ref, partner_ref, first_ref, second_ref, *outs):
+    count = first_ref.shape[0]
+    rows = jnp.concatenate([first_ref[...], second_ref[...]], axis=0)
+    total = product(rows, weight_ref, partner_ref)
+    outs[0][...] = halves(total[:count])
+    outs[1][...] = halves(total[count:])
+
+
+def first_product_kernel(weight_ref, partner_ref, bias_ref, *refs):
+    sources, (train_ref, near_ref, far_ref), refs = refs[:4], refs[4:7], refs[7:]
+    outs, train_out, kept_ref, far_out = refs[:4], refs[4], refs[5], refs[6]
     rows = sources[0].shape[0] - 1
-    count = 2 * rows
+    count, tokens = 2 * rows, train_ref.shape[0]
     slabs = [ref[:rows].reshape(count, ref.shape[-1]) for ref in sources]
+    slabs = slabs + [train_ref[...], near_ref[...], far_ref[...]]
     total = product(jnp.concatenate(slabs, axis=0), weight_ref, partner_ref)
     parts = [total[index * count : (index + 1) * count] for index in range(4)]
     parts[0] = parts[0] + bias_ref[...]
     outs[0][...] = parts[0]
     parts = [halves(part) for part in parts]
+    train_out[...] = total[4 * count : 4 * count + tokens] + bias_ref[...]
+    part = halves(total[4 * count + tokens :])
+    middle = tokens // 2
+    start = half() * middle
+    far_out[pl.ds(pl.multiple_of(start, 16), middle)] = part[:middle]
+    far_out[pl.ds(pl.multiple_of(middle - start, 16), middle)] = part[middle:]
     _, chip = place()
     row = lax.broadcasted_iota(jnp.int32, (64, 1), 0)
     mask, core, seen, token = row // 16, (row // 8) % 2, (row // 2) % 4, row % 2
@@ -218,7 +216,7 @@
     moved = moved.astype(jnp.bfloat16)
     for index in range(1, 4):
         outs[index][:count] = parts[index]
-        outs[index][count:] = moved[16 * index : 16 * (index + 1)]
+        outs[index][count : count + 16] = moved[16 * index : 16 * (index + 1)]
 
 
 def pick(target_ref, fresh, shards):
@@ -286,9 +284,17 @@
 
 
 def paired_train_kernel(
-    q_ref, document_ref, same_ref, other_ref, own_ref, *refs
+    q_ref, document_ref, decoded_ref, same_ref, other_ref, own_ref, *refs
 ):
-    sources, (train_ref, handover_ref) = refs[:-2], refs[-2:]
+    sources, refs = refs[:3], refs[3:]
+    decoded_hbm, train_hbm, handover_hbm, train_ref, handover_ref, sems = refs
+    copies = [
+        pltpu.make_async_copy(source, target, sems.at[index])
+        for index, (source, target) in enumerate(
+            ((decoded_ref, decoded_hbm), (handover_ref, handover_hbm))
+        )
+    ]
+    copies[0].start()
     core, chip = place()
     for source, ref in ((core, same_ref), (1 - core, other_ref)):
         rows = ref[...].astype(jnp.float32)
@@ -296,17 +302,32 @@
         for mask in range(4):
             pair = rows[2 * mask : 2 * mask + 2].astype(jnp.bfloat16)
             handover_ref[2 * (chip ^ mask) + source] = pair
+    copies[1].start()
     total = own_ref[...]
     for ref in sources:
         total = total + widened(ref[...])
-    train_attend(q_ref, document_ref, total.astype(jnp.bfloat16), train_ref)
+
+    def finish(head):
+        lanes = pl.ds(head * GROUP * HEAD_DIM, GROUP * HEAD_DIM)
+        copies.append(
+            pltpu.make_async_copy(
+                train_ref.at[:, lanes], train_hbm.at[:, lanes], sems.at[2 + head]
+            )
+        )
+        copies[-1].start()
+
+    train_attend(q_ref, document_ref, total.astype(jnp.bfloat16), train_ref, finish)
+    for copy in copies:
+        copy.wait()
 
 
 def train_kernel(q_ref, document_ref, own_ref, train_ref):
-    train_attend(q_ref, document_ref, own_ref[...].astype(jnp.bfloat16), train_ref)
-
-
-def train_attend(q_ref, document_ref, keys_values, train_ref):
+    train_attend(
+        q_ref, document_ref, own_ref[...].astype(jnp.bfloat16), train_ref, lambda head: None
+    )
+
+
+def train_attend(q_ref, document_ref, keys_values, train_ref, finish):
     tokens = q_ref.shape[0]
     local_kv = keys_values.shape[1] // (2 * HEAD_DIM)
     row = lax.broadcasted_iota(jnp.int32, (tokens, tokens), 0)
@@ -331,6 +352,7 @@
         for part in range(GROUP):
             lane = (head * GROUP + part) * HEAD_DIM
             train_ref[:, lane : lane + HEAD_DIM] = result[part * tokens : (part + 1) * tokens]
+        finish(head)
 
 
 def exchange(parts, core_groups):
@@ -339,14 +361,15 @@
     )
 
 
-def call(kernel, outs, *operands, in_place=0, room=12, **options):
+def call(kernel, outs, *operands, in_place=0, out_place=False, room=12, **options):
     single = not isinstance(outs, tuple)
     left = len(operands) - in_place
+    out_spec = HBM_SPEC if out_place else VMEM_SPEC
     return pl.pallas_call(
         kernel,
         out_shape=outs,
         in_specs=[HBM_SPEC] * in_place + [VMEM_SPEC] * left,
-        out_specs=VMEM_SPEC if single else (VMEM_SPEC,) * len(outs),
+        out_specs=out_spec if single else (out_spec,) * len(outs),
         compiler_params=pltpu.CompilerParams(vmem_limit_bytes=room << 20),
         **options,
     )(
@@ -422,12 +445,6 @@
 
         wide = columns * 3 // 2
 
-        def products(kernel, sources, rows, extra):
-            outs = [shape((rows, columns), jnp.float32)] + [shape((rows + extra, wide))] * 3
-            if extra:
-                outs.append(shape((extra, columns), jnp.float32))
-            return call(kernel, tuple(outs), project_weight, partner_weight, bias, *sources)
-
         others = (1, 2, 3)
         *slabs, bias, pack = call(
             slab_kernel,
@@ -449,31 +466,57 @@
         new_slabs, train_slabs = slabs[:4], slabs[4:]
         new_rows = [hop(new_slabs[mask], mask) for mask in others]
         train_rows = [hop(train_slabs[mask], mask) for mask in others]
-        own, first, second, third, kept = products(
-            new_product_kernel, [new_slabs[0]] + new_rows, fresh_count, 16
+        far = lax.ppermute(train_rows[2], "tensor", [(i, i ^ 1) for i in range(beside)])
+        weights = (project_weight, partner_weight)
+        own_type = shape((fresh_count, columns), jnp.float32)
+        sum_type = shape((train_count, columns), jnp.float32)
+        message = fresh_count + 16
+        own, first, second, third, train_own, kept, far_part = call(
+            first_product_kernel,
+            (
+                own_type,
+                shape((message, wide)),
+                shape((message, wide)),
+                shape((message, wide)),
+                sum_type,
+                shape((16, columns), jnp.float32),
+                shape((train_count, wide)),
+            ),
+            *weights,
+            bias,
+            new_slabs[0],
+            *new_rows,
+            train_slabs[0],
+            train_rows[2],
+            far,
         )
         back = [hop(part, mask) for mask, part in zip(others, (first, second, third))]
+        first, second = call(
+            second_product_kernel, (shape((train_count, wide)),) * 2, *weights, *train_rows[:2]
+        )
+        train_back = [hop(part, mask) for mask, part in zip(others, (first, second, far_part))]
         fresh, same = call(
             paired_fresh_kernel, (fresh_type, shape((16, columns))), own, kept, *back
         )
         other = swap(same)
-        far = lax.ppermute(train_rows[2], "tensor", [(i, i ^ 1) for i in range(beside)])
-        train_own, first, second, third = products(
-            train_product_kernel, [train_slabs[0]] + train_rows + [far], train_count, 0
-        )
-        train_back = [hop(part, mask) for mask, part in zip(others, (first, second, third))]
         decoded = call(decode_kernel, decoded_type, fresh, *decode_state)
-        train_attention, handover = call(
+        return call(
             paired_train_kernel,
-            (train_type, outgoing_type),
+            (decoded_type, train_type, outgoing_type),
             train_queries,
             pack,
+            decoded,
             same,
             other,
             train_own,
             *train_back,
-        )
-        return (decoded, train_attention, handover)
+            out_place=True,
+            scratch_shapes=[
+                pltpu.VMEM(train_queries.shape, jnp.bfloat16),
+                pltpu.VMEM((size, 2, columns), jnp.bfloat16),
+                pltpu.SemaphoreType.DMA((2 + local_kv,)),
+            ],
+        )
 
     def gathered(hidden):
         rows = hidden.reshape(-1, chips, 2 * depth)

time: 42.8 us -> 42.3 us (0.988)
  Pallas kernels: 9.83 us -> 9.12 us
    pallas_call x7, Pallas kernels: 9.83 us -> 9.12 us  [call(): pl.pallas_call(kernel, out_shape=outs, in_specs=[HBM_SPEC] * in_place + [...]
  transfers between devices with their start and end apart: 15 -> 15, of which waited for: 5 -> 4; matrix products, arithmetic and copies ran while one was open for 0% -> 0% of each run, Pallas kernels for 20% -> 18%
where the time goes in v2:
time: 42.3 us; the launch traced here: 42.1 us
  starting transfers between devices  19.1 us (45%)
  waiting for transfers between devices  13.1 us (31%)
  Pallas kernels  9.12 us (22%)
  between operations  0.75 us (2%)
    ppermute x12, starting transfers between devices, hop(): return lax.ppermute(value, 'fsdp', [(i, i ^ 2 * mask) for i in range(size)])  16.9 us
    ppermute x12, waiting for transfers between devices, hop(): return lax.ppermute(value, 'fsdp', [(i, i ^ 2 * mask) for i in range(size)])  13.1 us
    pallas_call x7, Pallas kernels, call(): pl.pallas_call(kernel, out_shape=outs, in_specs=[HBM_SPEC] * in_place + [...  9.12 us
    ppermute x1, starting transfers between devices, steps(): lax.ppermute(train_rows[2], 'tensor', [(i, i ^ 1) for i in range(beside)])  1.58 us
  transfers between devices with their start and end apart: 15, of which 4 were waited for; matrix products, arithmetic and copies ran while one was open for 0% of the time, Pallas kernels for 18%

profile of v2, /device:TPU:0, one launch (start us, length us, event | category | flops | bytes accessed | tf_op | source)
XLA Modules:
  0.0 42.1 jit_solution(17996527002993180527)
XLA Ops:
  0.6 0.6 %collective-permute-start = (bf16[1024,512]{1,0:T(8,128)(2,1)}, bf16[1024,512]{1,0:T(8,128)(2,1)S(1)}, u32[]{:S(2)}, u32[]{:S(2)}) collective-permute-start(bf16[1024,512]{1,0:T(8,128)(2,1)} %weight_ref.3), channel_id=1, source_target_pairs={{0,4},{4,0},{8,12},{12,8},{16,20},{20,16},{24,28},{28,24},{1,5},{5... | collective-permute-start | bytes 3145736 | tf_op jit(solution)/shard_map/ppermute | solution.py:401
  1.2 1.5 %shard_map.130 = (bf16[17,2,2048]{2,1,0:T(2,128)(2,1)S(1)}, bf16[17,2,2048]{2,1,0:T(2,128)(2,1)S(1)}, bf16[17,2,2048]{2,1,0:T(2,128)(2,1)S(1)}, bf16[17,2,2048]{...) custom-call(bf16[16,2,8192]{2,1,0:T(2,128)(2,1)} %new_hbm.1, ...), custom_call_target="tpu_custom_call" | custom-call | tf_op jit(solution)/shard_map/pallas_call | solution.py:368
  2.7 3.6 %collective-permute-start.4 = (bf16[32,2048]{1,0:T(8,128)(2,1)S(1)}, bf16[32,2048]{1,0:T(8,128)(2,1)S(1)}, u32[]{:S(2)}, u32[]{:S(2)}) collective-permute-start(bf16[32,2048]{1,0:T(8,128)(2,1)S(1)} %get-tuple-element.35), channel_id=1, source_target_pairs={{0,24},{4,28},{8,16},{12,20},{16,8},{20,12},{24,0},{28,4},{1,25},{... | collective-permute-start | bytes 393224 | tf_op jit(solution)/shard_map/ppermute | solution.py:444
  6.3 0.5 %collective-permute-start.1 = (bf16[17,2,2048]{2,1,0:T(2,128)(2,1)S(1)}, bf16[17,2,2048]{2,1,0:T(2,128)(2,1)S(1)}, u32[]{:S(2)}, u32[]{:S(2)}) collective-permute-start(bf16[17,2,2048]{2,1,0:T(2,128)(2,1)S(1)} %get-tuple-element.31), channel_id=1, source_target_pairs={{0,8},{4,12},{8,0},{12,4},{16,24},{20,28},{24,16},{28,20},{1,9},{5... | collective-permute-start | bytes 417800 | tf_op jit(solution)/shard_map/ppermute | solution.py:444
  6.8 0.1 collective-permute-start.2
  7.0 1.9 %collective-permute-start.10 = (bf16[64,2048]{1,0:T(8,128)(2,1)S(1)}, bf16[64,2048]{1,0:T(8,128)(2,1)S(1)}, u32[]{:S(2)}, u32[]{:S(2)}) collective-permute-start(bf16[64,2048]{1,0:T(8,128)(2,1)S(1)} %get-tuple-element.48), channel_id=1, source_target_pairs={{0,8},{4,12},{8,0},{12,4},{16,24},{20,28},{24,16},{28,20},{1,9},{5... | collective-permute-start | bytes 786440 | tf_op jit(solution)/shard_map/ppermute | solution.py:444
  8.8 1.8 %collective-permute-done.4.refs_5_ = bf16[32,2048]{1,0:T(8,128)(2,1)S(1)} collective-permute-done((bf16[32,2048]{1,0:T(8,128)(2,1)S(1)}, bf16[32,2048]{1,0:T(8,128)(2,1)S(1)}, u32[]{:S(2)}, u32[]{:S(2)}) %collective-permute-start.4) | collective-permute-done | bytes 131104 | tf_op jit(solution)/shard_map/ppermute | solution.py:444
  10.7 2.0 %collective-permute-start.11 = (bf16[64,2048]{1,0:T(8,128)(2,1)S(1)}, bf16[64,2048]{1,0:T(8,128)(2,1)S(1)}, u32[]{:S(2)}, u32[]{:S(2)}) collective-permute-start(bf16[64,2048]{1,0:T(8,128)(2,1)S(1)} %get-tuple-element.49), channel_id=1, source_target_pairs={{0,16},{4,20},{8,24},{12,28},{16,0},{20,4},{24,8},{28,12},{1,17},{... | collective-permute-start | bytes 786440 | tf_op jit(solution)/shard_map/ppermute | solution.py:444
  12.7 1.5 %collective-permute-done.1.refs_1_ = bf16[17,2,2048]{2,1,0:T(2,128)(2,1)S(1)} collective-permute-done((bf16[17,2,2048]{2,1,0:T(2,128)(2,1)S(1)}, bf16[17,2,2048]{2,1,0:T(2,128)(2,1)S(1)}, u32[]{:S(2)}, u32[]{:S(2)}) %collective-permute-start.1) | collective-permute-done | bytes 139296 | tf_op jit(solution)/shard_map/ppermute | solution.py:444
  14.2 1.4 %collective-permute-start.3 = (bf16[17,2,2048]{2,1,0:T(2,128)(2,1)S(1)}, bf16[17,2,2048]{2,1,0:T(2,128)(2,1)S(1)}, u32[]{:S(2)}, u32[]{:S(2)}) collective-permute-start(bf16[17,2,2048]{2,1,0:T(2,128)(2,1)S(1)} %get-tuple-element.33), channel_id=1, source_target_pairs={{0,24},{4,28},{8,16},{12,20},{16,8},{20,12},{24,0},{28,4},{1,25},{... | collective-permute-start | bytes 417800 | tf_op jit(solution)/shard_map/ppermute | solution.py:444
  15.6 1.6 %collective-permute-start.5 = (bf16[32,2048]{1,0:T(8,128)(2,1)S(1)}, bf16[32,2048]{1,0:T(8,128)(2,1)S(1)}, u32[]{:S(2)}, u32[]{:S(2)}) collective-permute-start(bf16[32,2048]{1,0:T(8,128)(2,1)S(1)} %collective-permute-done.4.refs_5_), channel_id=1, source_target_pairs={{0,1},{1,0},{2,3},{3,2},{4,5},{5,4},{6,7},{7,6},{8,9},{9,8},{10,11... | collective-permute-start | bytes 393224 | tf_op jit(solution)/shard_map/ppermute | solution.py:469
  17.2 4.8 %collective-permute-done.3.refs_3_ = bf16[17,2,2048]{2,1,0:T(2,128)(2,1)S(1)} collective-permute-done((bf16[17,2,2048]{2,1,0:T(2,128)(2,1)S(1)}, bf16[17,2,2048]{2,1,0:T(2,128)(2,1)S(1)}, u32[]{:S(2)}, u32[]{:S(2)}) %collective-permute-start.3) | collective-permute-done | bytes 139296 | tf_op jit(solution)/shard_map/ppermute | solution.py:444
  22.0 1.0 %shard_map.131 = (f32[32,512]{1,0:T(8,128)S(1)}, bf16[48,768]{1,0:T(8,128)(2,1)S(1)}, bf16[48,768]{1,0:T(8,128)(2,1)S(1)}, bf16[48,768]{1,0:T(8,128)(2,1)S(1)}, ...) custom-call(bf16[1024,512]{1,0:T(8,128)(2,1)S(1)} %copy-done, ...), custom_call_target="tpu_custom_call" | custom-call | tf_op jit(solution)/shard_map/pallas_call | solution.py:368
  23.0 1.7 %collective-permute-start.6 = (bf16[48,768]{1,0:T(8,128)(2,1)S(1)}, bf16[48,768]{1,0:T(8,128)(2,1)S(1)}, u32[]{:S(2)}, u32[]{:S(2)}) collective-permute-start(bf16[48,768]{1,0:T(8,128)(2,1)S(1)} %get-tuple-element.38), channel_id=1, source_target_pairs={{0,8},{4,12},{8,0},{12,4},{16,24},{20,28},{24,16},{28,20},{1,9},{5... | collective-permute-start | bytes 221192 | tf_op jit(solution)/shard_map/ppermute | solution.py:444
  24.7 1.5 %collective-permute-start.14 = (bf16[64,768]{1,0:T(8,128)(2,1)S(1)}, bf16[64,768]{1,0:T(8,128)(2,1)S(1)}, u32[]{:S(2)}, u32[]{:S(2)}) collective-permute-start(bf16[64,768]{1,0:T(8,128)(2,1)S(1)} %get-tuple-element.52), channel_id=1, source_target_pairs={{0,24},{4,28},{8,16},{12,20},{16,8},{20,12},{24,0},{28,4},{1,25},{... | collective-permute-start | bytes 294920 | tf_op jit(solution)/shard_map/ppermute | solution.py:444
  26.3 0.5 %shard_map.135 = (bf16[64,768]{1,0:T(8,128)(2,1)S(1)}, bf16[64,768]{1,0:T(8,128)(2,1)S(1)}) custom-call(bf16[1024,512]{1,0:T(8,128)(2,1)S(1)} %copy-done, bf16[1024,512]{1,0:T(8,128)(2,1)S(1)} %collective-permute-done.partner_ref, bf16[64,2048]{1,0:T(8,128)(2,1)S(1)} %collective-permute-done.10.first_ref, bf16[64,2048]{1,0:T(8,128)(2,1)S(1)} %collective-permute-done.11.second_ref), custom_call_target="tpu_custom_call" | custom-call | tf_op jit(solution)/shard_map/pallas_call | solution.py:368
  26.8 1.5 %collective-permute-start.12 = (bf16[64,768]{1,0:T(8,128)(2,1)S(1)}, bf16[64,768]{1,0:T(8,128)(2,1)S(1)}, u32[]{:S(2)}, u32[]{:S(2)}) collective-permute-start(bf16[64,768]{1,0:T(8,128)(2,1)S(1)} %get-tuple-element.50), channel_id=1, source_target_pairs={{0,8},{4,12},{8,0},{12,4},{16,24},{20,28},{24,16},{28,20},{1,9},{5... | collective-permute-start | bytes 294920 | tf_op jit(solution)/shard_map/ppermute | solution.py:444
  28.3 0.5 %collective-permute-start.13 = (bf16[64,768]{1,0:T(8,128)(2,1)S(1)}, bf16[64,768]{1,0:T(8,128)(2,1)S(1)}, u32[]{:S(2)}, u32[]{:S(2)}) collective-permute-start(bf16[64,768]{1,0:T(8,128)(2,1)S(1)} %get-tuple-element.51), channel_id=1, source_target_pairs={{0,16},{4,20},{8,24},{12,28},{16,0},{20,4},{24,8},{28,12},{1,17},{... | collective-permute-start | bytes 294920 | tf_op jit(solution)/shard_map/ppermute | solution.py:444
  28.8 1.6 %collective-permute-start.7 = (bf16[48,768]{1,0:T(8,128)(2,1)S(1)}, bf16[48,768]{1,0:T(8,128)(2,1)S(1)}, u32[]{:S(2)}, u32[]{:S(2)}) collective-permute-start(bf16[48,768]{1,0:T(8,128)(2,1)S(1)} %get-tuple-element.39), channel_id=1, source_target_pairs={{0,16},{4,20},{8,24},{12,28},{16,0},{20,4},{24,8},{28,12},{1,17},{... | collective-permute-start | bytes 221192 | tf_op jit(solution)/shard_map/ppermute | solution.py:444
  30.3 0.5 %collective-permute-start.8 = (bf16[48,768]{1,0:T(8,128)(2,1)S(1)}, bf16[48,768]{1,0:T(8,128)(2,1)S(1)}, u32[]{:S(2)}, u32[]{:S(2)}) collective-permute-start(bf16[48,768]{1,0:T(8,128)(2,1)S(1)} %get-tuple-element.40), channel_id=1, source_target_pairs={{0,24},{4,28},{8,16},{12,20},{16,8},{20,12},{24,0},{28,4},{1,25},{... | collective-permute-start | bytes 221192 | tf_op jit(solution)/shard_map/ppermute | solution.py:444
  30.9 5.0 %collective-permute-done.7.refs_1_ = bf16[48,768]{1,0:T(8,128)(2,1)S(1)} collective-permute-done((bf16[48,768]{1,0:T(8,128)(2,1)S(1)}, bf16[48,768]{1,0:T(8,128)(2,1)S(1)}, u32[]{:S(2)}, u32[]{:S(2)}) %collective-permute-start.7) | collective-permute-done | bytes 73760 | tf_op jit(solution)/shard_map/ppermute | solution.py:444
  35.9 3.9 %shard_map.133 = (bf16[16,2,2048]{2,1,0:T(2,128)(2,1)S(1)}, f32[2,256,128]{2,1,0:T(8,128)S(1)}, f32[2,256,128]{2,1,0:T(8,128)S(1)}, f32[2,256,128]{2,1,0:T(8,128)S(1)}) custom-call(bf16[16,2,2048]{2,1,0:T(2,128)(2,1)} %q_hbm.1, bf16[2048,512]{1,0:T(8,128)(2,1)} %bitcast.5, s32[8,16]{1,0:T(8,128)} %bitcast.6, s32[1,16]{1,0:T(1,128)} %bitcast.9), custom_call_target="tpu_custom_call" | custom-call | tf_op jit(solution)/shard_map/pallas_call | solution.py:368
  39.9 0.8 %shard_map.134.decoded_ref = bf16[16,2,2048]{2,1,0:T(2,128)(2,1)S(1)} custom-call(bf16[32,512]{1,0:T(8,128)(2,1)S(1)} %get-tuple-element.41.fresh_ref, bf16[16,2,2048]{2,1,0:T(2,128)(2,1)S(1)} %get-tuple-element.42.q_ref, f32[2,256,128]{2,1,0:T(8,128)S(1)} %get-tuple-element.43.acc_ref, f32[2,256,128]{2,1,0:T(8,128)S(1)} %get-tuple-element.44.top_ref, ...), custom_call_target="tpu_custom_call" | custom-call | tf_op jit(solution)/shard_map/pallas_call | solution.py:368
  40.7 1.4 %shard_map.136 = (bf16[16,2,2048]{2,1,0:T(2,128)(2,1)}, bf16[64,2048]{1,0:T(8,128)(2,1)}, bf16[8,2,512]{2,1,0:T(2,128)(2,1)}) custom-call(bf16[64,2048]{1,0:T(8,128)(2,1)S(1)} %copy-done.1, s32[1,64]{1,0:T(1,128)S(1)} %get-tuple-element.28.document_ref, bf16[16,2,2048]{2,1,0:T(2,128)(2,1)S(1)} %shard_map.134.decoded_ref, ...), custom_call_target="tpu_custom_call" | custom-call | tf_op jit(solution)/shard_map/pallas_call | solution.py:368
  (17 shorter events, 0.2 us)
Async XLA Ops:
  0.6 21.4 %copy-start = (bf16[1024,512]{1,0:T(8,128)(2,1)S(1)}, bf16[1024,512]{1,0:T(8,128)(2,1)}, u32[]{:S(2)}) copy-start(bf16[1024,512]{1,0:T(8,128)(2,1)} %weight_ref.3) | copy-start | bytes 3145732
  0.6 21.3 %collective-permute-start = (bf16[1024,512]{1,0:T(8,128)(2,1)}, bf16[1024,512]{1,0:T(8,128)(2,1)S(1)}, u32[]{:S(2)}, u32[]{:S(2)}) collective-permute-start(bf16[1024,512]{1,0:T(8,128)(2,1)} %weight_ref.3), channel_id=1, source_target_pairs={{0,4},{4,0},{8,12},{12,8},{16,20},{20,16},{24,28},{28,24},{1,5},{5... | collective-permute-start | bytes 3145736 | tf_op jit(solution)/shard_map/ppermute | solution.py:401
  2.7 7.9 %collective-permute-start.4 = (bf16[32,2048]{1,0:T(8,128)(2,1)S(1)}, bf16[32,2048]{1,0:T(8,128)(2,1)S(1)}, u32[]{:S(2)}, u32[]{:S(2)}) collective-permute-start(bf16[32,2048]{1,0:T(8,128)(2,1)S(1)} %get-tuple-element.35), channel_id=1, source_target_pairs={{0,24},{4,28},{8,16},{12,20},{16,8},{20,12},{24,0},{28,4},{1,25},{... | collective-permute-start | bytes 393224 | tf_op jit(solution)/shard_map/ppermute | solution.py:444
  6.3 7.9 %collective-permute-start.1 = (bf16[17,2,2048]{2,1,0:T(2,128)(2,1)S(1)}, bf16[17,2,2048]{2,1,0:T(2,128)(2,1)S(1)}, u32[]{:S(2)}, u32[]{:S(2)}) collective-permute-start(bf16[17,2,2048]{2,1,0:T(2,128)(2,1)S(1)} %get-tuple-element.31), channel_id=1, source_target_pairs={{0,8},{4,12},{8,0},{12,4},{16,24},{20,28},{24,16},{28,20},{1,9},{5... | collective-permute-start | bytes 417800 | tf_op jit(solution)/shard_map/ppermute | solution.py:444
  6.8 8.8 %collective-permute-start.2 = (bf16[17,2,2048]{2,1,0:T(2,128)(2,1)S(1)}, bf16[17,2,2048]{2,1,0:T(2,128)(2,1)S(1)}, u32[]{:S(2)}, u32[]{:S(2)}) collective-permute-start(bf16[17,2,2048]{2,1,0:T(2,128)(2,1)S(1)} %get-tuple-element.32), channel_id=1, source_target_pairs={{0,16},{4,20},{8,24},{12,28},{16,0},{20,4},{24,8},{28,12},{1,17},{... | collective-permute-start | bytes 417800 | tf_op jit(solution)/shard_map/ppermute | solution.py:444
  7.0 19.3 %collective-permute-start.10 = (bf16[64,2048]{1,0:T(8,128)(2,1)S(1)}, bf16[64,2048]{1,0:T(8,128)(2,1)S(1)}, u32[]{:S(2)}, u32[]{:S(2)}) collective-permute-start(bf16[64,2048]{1,0:T(8,128)(2,1)S(1)} %get-tuple-element.48), channel_id=1, source_target_pairs={{0,8},{4,12},{8,0},{12,4},{16,24},{20,28},{24,16},{28,20},{1,9},{5... | collective-permute-start | bytes 786440 | tf_op jit(solution)/shard_map/ppermute | solution.py:444
  10.7 15.6 %collective-permute-start.11 = (bf16[64,2048]{1,0:T(8,128)(2,1)S(1)}, bf16[64,2048]{1,0:T(8,128)(2,1)S(1)}, u32[]{:S(2)}, u32[]{:S(2)}) collective-permute-start(bf16[64,2048]{1,0:T(8,128)(2,1)S(1)} %get-tuple-element.49), channel_id=1, source_target_pairs={{0,16},{4,20},{8,24},{12,28},{16,0},{20,4},{24,8},{28,12},{1,17},{... | collective-permute-start | bytes 786440 | tf_op jit(solution)/shard_map/ppermute | solution.py:444
  14.2 7.8 %collective-permute-start.3 = (bf16[17,2,2048]{2,1,0:T(2,128)(2,1)S(1)}, bf16[17,2,2048]{2,1,0:T(2,128)(2,1)S(1)}, u32[]{:S(2)}, u32[]{:S(2)}) collective-permute-start(bf16[17,2,2048]{2,1,0:T(2,128)(2,1)S(1)} %get-tuple-element.33), channel_id=1, source_target_pairs={{0,24},{4,28},{8,16},{12,20},{16,8},{20,12},{24,0},{28,4},{1,25},{... | collective-permute-start | bytes 417800 | tf_op jit(solution)/shard_map/ppermute | solution.py:444
  15.6 6.4 %collective-permute-start.5 = (bf16[32,2048]{1,0:T(8,128)(2,1)S(1)}, bf16[32,2048]{1,0:T(8,128)(2,1)S(1)}, u32[]{:S(2)}, u32[]{:S(2)}) collective-permute-start(bf16[32,2048]{1,0:T(8,128)(2,1)S(1)} %collective-permute-done.4.refs_5_), channel_id=1, source_target_pairs={{0,1},{1,0},{2,3},{3,2},{4,5},{5,4},{6,7},{7,6},{8,9},{9,8},{10,11... | collective-permute-start | bytes 393224 | tf_op jit(solution)/shard_map/ppermute | solution.py:469
  23.0 7.3 %collective-permute-start.6 = (bf16[48,768]{1,0:T(8,128)(2,1)S(1)}, bf16[48,768]{1,0:T(8,128)(2,1)S(1)}, u32[]{:S(2)}, u32[]{:S(2)}) collective-permute-start(bf16[48,768]{1,0:T(8,128)(2,1)S(1)} %get-tuple-element.38), channel_id=1, source_target_pairs={{0,8},{4,12},{8,0},{12,4},{16,24},{20,28},{24,16},{28,20},{1,9},{5... | collective-permute-start | bytes 221192 | tf_op jit(solution)/shard_map/ppermute | solution.py:444
  24.7 16.0 %collective-permute-start.14 = (bf16[64,768]{1,0:T(8,128)(2,1)S(1)}, bf16[64,768]{1,0:T(8,128)(2,1)S(1)}, u32[]{:S(2)}, u32[]{:S(2)}) collective-permute-start(bf16[64,768]{1,0:T(8,128)(2,1)S(1)} %get-tuple-element.52), channel_id=1, source_target_pairs={{0,24},{4,28},{8,16},{12,20},{16,8},{20,12},{24,0},{28,4},{1,25},{... | collective-permute-start | bytes 294920 | tf_op jit(solution)/shard_map/ppermute | solution.py:444
  26.7 14.0 %copy-start.1 = (bf16[64,2048]{1,0:T(8,128)(2,1)S(1)}, bf16[64,2048]{1,0:T(8,128)(2,1)}, u32[]{:S(2)}) copy-start(bf16[64,2048]{1,0:T(8,128)(2,1)} %q_ref.1) | copy-start | bytes 786436
  26.8 14.0 %collective-permute-start.12 = (bf16[64,768]{1,0:T(8,128)(2,1)S(1)}, bf16[64,768]{1,0:T(8,128)(2,1)S(1)}, u32[]{:S(2)}, u32[]{:S(2)}) collective-permute-start(bf16[64,768]{1,0:T(8,128)(2,1)S(1)} %get-tuple-element.50), channel_id=1, source_target_pairs={{0,8},{4,12},{8,0},{12,4},{16,24},{20,28},{24,16},{28,20},{1,9},{5... | collective-permute-start | bytes 294920 | tf_op jit(solution)/shard_map/ppermute | solution.py:444
  28.3 12.4 %collective-permute-start.13 = (bf16[64,768]{1,0:T(8,128)(2,1)S(1)}, bf16[64,768]{1,0:T(8,128)(2,1)S(1)}, u32[]{:S(2)}, u32[]{:S(2)}) collective-permute-start(bf16[64,768]{1,0:T(8,128)(2,1)S(1)} %get-tuple-element.51), channel_id=1, source_target_pairs={{0,16},{4,20},{8,24},{12,28},{16,0},{20,4},{24,8},{28,12},{1,17},{... | collective-permute-start | bytes 294920 | tf_op jit(solution)/shard_map/ppermute | solution.py:444
  28.8 7.0 %collective-permute-start.7 = (bf16[48,768]{1,0:T(8,128)(2,1)S(1)}, bf16[48,768]{1,0:T(8,128)(2,1)S(1)}, u32[]{:S(2)}, u32[]{:S(2)}) collective-permute-start(bf16[48,768]{1,0:T(8,128)(2,1)S(1)} %get-tuple-element.39), channel_id=1, source_target_pairs={{0,16},{4,20},{8,24},{12,28},{16,0},{20,4},{24,8},{28,12},{1,17},{... | collective-permute-start | bytes 221192 | tf_op jit(solution)/shard_map/ppermute | solution.py:444
  30.3 5.5 %collective-permute-start.8 = (bf16[48,768]{1,0:T(8,128)(2,1)S(1)}, bf16[48,768]{1,0:T(8,128)(2,1)S(1)}, u32[]{:S(2)}, u32[]{:S(2)}) collective-permute-start(bf16[48,768]{1,0:T(8,128)(2,1)S(1)} %get-tuple-element.40), channel_id=1, source_target_pairs={{0,24},{4,28},{8,16},{12,20},{16,8},{20,12},{24,0},{28,4},{1,25},{... | collective-permute-start | bytes 221192 | tf_op jit(solution)/shard_map/ppermute | solution.py:444
  35.9 4.8 %collective-permute-start.9 = (bf16[16,512]{1,0:T(8,128)(2,1)S(1)}, bf16[16,512]{1,0:T(8,128)(2,1)S(1)}, u32[]{:S(2)}, u32[]{:S(2)}) collective-permute-start(bf16[16,512]{1,0:T(8,128)(2,1)S(1)} %get-tuple-element.46.same_ref), channel_id=1, source_target_pairs={{0,4},{4,0},{8,12},{12,8},{16,20},{20,16},{24,28},{28,24},{1,5},{5... | collective-permute-start | bytes 49160 | tf_op jit(solution)/shard_map/ppermute | solution.py:401

commit v3 on v2

--- a/solution.py
+++ b/solution.py
@@ -47,6 +47,28 @@
     )
 
 
+def paired_cached_kernel(
+    page, q_hbm, cache_hbm, table_hbm, length_hbm, new_hbm, train_hbm, bias_hbm, target_hbm,
+    document_hbm, q_ref, acc_ref, top_ref, total_ref, new_ref, train_ref, bias_ref, target_ref,
+    document_ref, cache_ref, table_ref, length_ref, count_ref, score_ref, sems, own_sems,
+):
+    width = new_ref.shape[-1]
+    pairs = (
+        (slab(new_hbm, 0, width), new_ref),
+        (slab(train_hbm, 0, width), train_ref),
+        (bias_hbm, bias_ref),
+        (target_hbm, target_ref),
+        (document_hbm, document_ref),
+    )
+    copies = all_started(pairs, own_sems)
+    cached_kernel(
+        page, q_hbm, cache_hbm, table_hbm, length_hbm, q_ref, acc_ref, top_ref, total_ref,
+        cache_ref, table_ref, length_ref, count_ref, score_ref, sems,
+    )
+    for copy in copies:
+        copy.wait()
+
+
 def cached_kernel(
     page, q_hbm, cache_hbm, table_hbm, length_hbm, q_ref, acc_ref, top_ref, total_ref,
     cache_ref, table_ref, length_ref, count_ref, score_ref, sems,
@@ -54,12 +76,7 @@
     pairs = (
         (table_hbm, table_ref), (length_hbm, length_ref), (q_hbm, q_ref), (cache_hbm, cache_ref)
     )
-    copies = [
-        pltpu.make_async_copy(source, target, sems.at[index])
-        for index, (source, target) in enumerate(pairs)
-    ]
-    for copy in copies:
-        copy.start()
+    copies = all_started(pairs, sems)
     for copy in copies[:2]:
         copy.wait()
     tokens, columns = cache_ref.shape
@@ -108,32 +125,38 @@
         total_ref[head] = jnp.broadcast_to(jnp.sum(total, axis=-1, keepdims=True), acc.shape)
 
 
-def slab_kernel(
-    new_hbm, train_hbm, target_hbm, bias_hbm, document_hbm, *refs
-):
-    slabs, (bias_ref, document_ref, target_ref, sems) = refs[:8], refs[8:]
-    rows = new_hbm.shape[0]
-    width = slabs[0].shape[-1]
+def slab(source, mask, width):
     _, chip = place()
-    copies = [pltpu.make_async_copy(target_hbm, target_ref, sems.at[0])]
-    for index, slab in enumerate(slabs):
-        start = pl.multiple_of((chip ^ (index % 4)) * width, 128)
-        if index < 4:
-            source, slab = new_hbm.at[:, :, pl.ds(start, width)], slab.at[pl.ds(0, rows)]
-        else:
-            count = slab.shape[0]
-            first = half() * count if index == 7 else 0
-            source = train_hbm.at[pl.ds(first, count), pl.ds(start, width)]
-        copies.append(pltpu.make_async_copy(source, slab, sems.at[1 + index]))
-    copies.append(pltpu.make_async_copy(bias_hbm, bias_ref, sems.at[9]))
-    copies.append(pltpu.make_async_copy(document_hbm, document_ref, sems.at[10]))
+    lanes = pl.ds(pl.multiple_of((chip ^ mask) * width, 128), width)
+    return source.at[:, :, lanes] if len(source.shape) == 3 else source.at[:, lanes]
+
+
+def all_started(pairs, sems):
+    copies = [
+        pltpu.make_async_copy(source, target, sems.at[index])
+        for index, (source, target) in enumerate(pairs)
+    ]
     for copy in copies:
         copy.start()
+    return copies
+
+
+def slab_kernel(new_hbm, train_hbm, target_hbm, *refs):
+    new_slabs, train_slabs, (target_ref, sems) = refs[:3], refs[3:6], refs[6:]
+    rows, width = new_hbm.shape[0], train_slabs[0].shape[-1]
+    count = train_slabs[2].shape[0]
+    pairs = [(target_hbm, target_ref)]
+    for mask, ref in enumerate(new_slabs, 1):
+        pairs.append((slab(new_hbm, mask, width), ref.at[pl.ds(0, rows)]))
+    for mask, ref in enumerate(train_slabs, 1):
+        source = train_hbm.at[pl.ds(half() * count, count)] if mask == 3 else train_hbm
+        pairs.append((slab(source, mask, width), ref))
+    copies = all_started(pairs, sems)
     copies[0].wait()
     target = target_ref[...].astype(jnp.float32).astype(jnp.bfloat16)
-    for slab in slabs[:4]:
-        slab[rows, :, :] = jnp.zeros((2, width), jnp.bfloat16)
-        slab[rows, :, 0:rows] = jnp.broadcast_to(target, (2, rows))
+    for ref in new_slabs:
+        ref[rows, :, :] = jnp.zeros((2, width), jnp.bfloat16)
+        ref[rows, :, 0:rows] = jnp.broadcast_to(target, (2, rows))
     for copy in copies[1:]:
         copy.wait()
 
@@ -145,6 +168,20 @@
         rest[:, start : start + HEAD_DIM] for start in range(0, total.shape[1], 2 * HEAD_DIM)
     ]
     return jnp.concatenate([whole] + keys, axis=1)
+
+
+def packed(parts, columns):
+    count = parts.shape[0] // 2
+    rests = parts[:, columns:]
+    rests = jnp.concatenate([rests[:count], rests[count:]], axis=1)
+    return jnp.concatenate([parts[:, :columns], rests], axis=0)
+
+
+def unpacked(rows):
+    count, columns = rows.shape[0] // 3, rows.shape[1]
+    rests = rows[2 * count :]
+    rests = jnp.concatenate([rests[:, : columns // 2], rests[:, columns // 2 :]], axis=0)
+    return widened(jnp.concatenate([rows[: 2 * count], rests], axis=1))
 
 
 def widened(parts):
@@ -178,11 +215,12 @@
     outs[1][...] = halves(total[count:])
 
 
-def first_product_kernel(weight_ref, partner_ref, bias_ref, *refs):
+def first_product_kernel(weight_ref, partner_ref, bias_ref, target_ref, *refs):
     sources, (train_ref, near_ref, far_ref), refs = refs[:4], refs[4:7], refs[7:]
     outs, train_out, kept_ref, far_out = refs[:4], refs[4], refs[5], refs[6]
-    rows = sources[0].shape[0] - 1
+    rows = sources[0].shape[0]
     count, tokens = 2 * rows, train_ref.shape[0]
+    columns = train_out.shape[1]
     slabs = [ref[:rows].reshape(count, ref.shape[-1]) for ref in sources]
     slabs = slabs + [train_ref[...], near_ref[...], far_ref[...]]
     total = product(jnp.concatenate(slabs, axis=0), weight_ref, partner_ref)
@@ -204,19 +242,24 @@
     lane = lax.broadcasted_iota(jnp.int32, (rows, count), 1)
     moved = None
     for index, ref in enumerate(sources):
-        target = ref[rows, :, 0:rows].astype(jnp.float32)[:1]
+        if index == 0:
+            target = target_ref[...].astype(jnp.float32)
+        else:
+            target = ref[rows, :, 0:rows].astype(jnp.float32)[:1]
         target = column_of(target, rows)
         target = jnp.sum(jnp.where(lane // 2 == entry, target, 0.0), axis=0, keepdims=True)
         chosen = (target == shard) & (token == lane[:1] % 2) & ((mask ^ seen) == index)
         picked = jnp.dot(
-            chosen.astype(jnp.bfloat16), parts[index], preferred_element_type=jnp.float32
+            chosen.astype(jnp.bfloat16),
+            parts[index][:, :columns],
+            preferred_element_type=jnp.float32,
         )
         moved = picked if moved is None else moved + picked
-    kept_ref[...] = widened(moved[:16])
+    kept_ref[...] = moved[:16]
     moved = moved.astype(jnp.bfloat16)
     for index in range(1, 4):
-        outs[index][:count] = parts[index]
-        outs[index][count : count + 16] = moved[16 * index : 16 * (index + 1)]
+        outs[index][: 3 * rows] = packed(parts[index], columns)
+        outs[index][3 * rows :] = moved[16 * index : 16 * (index + 1)]
 
 
 def pick(target_ref, fresh, shards):
@@ -244,9 +287,8 @@
     count = own_ref.shape[0]
     fresh, moved = own_ref[...], kept_ref[...]
     for ref in sources:
-        arrived = widened(ref[...])
-        fresh = fresh + arrived[:count]
-        moved = moved + arrived[count:]
+        fresh = fresh + unpacked(ref[: count * 3 // 2])
+        moved = moved + ref[count * 3 // 2 :].astype(jnp.float32)
     fresh_ref[...] = fresh.astype(jnp.bfloat16)
     moved_ref[...] = moved.astype(jnp.bfloat16)
 
@@ -283,18 +325,10 @@
             )
 
 
-def paired_train_kernel(
-    q_ref, document_ref, decoded_ref, same_ref, other_ref, own_ref, *refs
+def settle_kernel(
+    document_ref, decoded_ref, same_ref, other_ref, own_ref, far_ref, decoded_hbm, handover_hbm,
+    sum_ref, allowed_ref, handover_ref, sems,
 ):
-    sources, refs = refs[:3], refs[3:]
-    decoded_hbm, train_hbm, handover_hbm, train_ref, handover_ref, sems = refs
-    copies = [
-        pltpu.make_async_copy(source, target, sems.at[index])
-        for index, (source, target) in enumerate(
-            ((decoded_ref, decoded_hbm), (handover_ref, handover_hbm))
-        )
-    ]
-    copies[0].start()
     core, chip = place()
     for source, ref in ((core, same_ref), (1 - core, other_ref)):
         rows = ref[...].astype(jnp.float32)
@@ -302,40 +336,53 @@
         for mask in range(4):
             pair = rows[2 * mask : 2 * mask + 2].astype(jnp.bfloat16)
             handover_ref[2 * (chip ^ mask) + source] = pair
-    copies[1].start()
-    total = own_ref[...]
-    for ref in sources:
-        total = total + widened(ref[...])
+    copies = all_started(((decoded_ref, decoded_hbm), (handover_ref, handover_hbm)), sems)
+    sum_ref[...] = own_ref[...] + widened(far_ref[...])
+    allowed_ref[...] = allowed_pairs(document_ref)
+    for copy in copies:
+        copy.wait()
+
+
+def paired_train_kernel(
+    q_ref, allowed_ref, own_ref, first_ref, second_ref, train_hbm, train_ref, sems
+):
+    copies = []
 
     def finish(head):
         lanes = pl.ds(head * GROUP * HEAD_DIM, GROUP * HEAD_DIM)
         copies.append(
-            pltpu.make_async_copy(
-                train_ref.at[:, lanes], train_hbm.at[:, lanes], sems.at[2 + head]
-            )
+            pltpu.make_async_copy(train_ref.at[:, lanes], train_hbm.at[:, lanes], sems.at[head])
         )
         copies[-1].start()
 
-    train_attend(q_ref, document_ref, total.astype(jnp.bfloat16), train_ref, finish)
+    total = own_ref[...] + widened(first_ref[...]) + widened(second_ref[...])
+    train_attend(q_ref, allowed_ref[...], total.astype(jnp.bfloat16), train_ref, finish)
     for copy in copies:
         copy.wait()
 
 
+def allowed_pairs(document_ref):
+    tokens = document_ref.shape[1]
+    row = lax.broadcasted_iota(jnp.int32, (tokens, tokens), 0)
+    column = lax.broadcasted_iota(jnp.int32, (tokens, tokens), 1)
+    allowed = (column <= row) & (document_ref[...] == column_of(document_ref[...], tokens))
+    return allowed.astype(jnp.float32)
+
+
 def train_kernel(q_ref, document_ref, own_ref, train_ref):
     train_attend(
-        q_ref, document_ref, own_ref[...].astype(jnp.bfloat16), train_ref, lambda head: None
-    )
-
-
-def train_attend(q_ref, document_ref, keys_values, train_ref, finish):
+        q_ref,
+        allowed_pairs(document_ref),
+        own_ref[...].astype(jnp.bfloat16),
+        train_ref,
+        lambda head: None,
+    )
+
+
+def train_attend(q_ref, allowed, keys_values, train_ref, finish):
     tokens = q_ref.shape[0]
     local_kv = keys_values.shape[1] // (2 * HEAD_DIM)
-    row = lax.broadcasted_iota(jnp.int32, (tokens, tokens), 0)
-    column = lax.broadcasted_iota(jnp.int32, (tokens, tokens), 1)
-    allowed = (column <= row) & (
-        document_ref[...] == column_of(document_ref[...], tokens)
-    )
-    allowed = jnp.concatenate([allowed.astype(jnp.float32)] * GROUP, axis=0) > 0.0
+    allowed = jnp.concatenate([allowed] * GROUP, axis=0) > 0.0
     for head in range(local_kv):
         base = head * 2 * HEAD_DIM
         middle, end = base + HEAD_DIM, base + 2 * HEAD_DIM
@@ -361,15 +408,15 @@
     )
 
 
-def call(kernel, outs, *operands, in_place=0, out_place=False, room=12, **options):
+def call(kernel, outs, *operands, in_place=0, out_place=0, room=12, **options):
     single = not isinstance(outs, tuple)
     left = len(operands) - in_place
-    out_spec = HBM_SPEC if out_place else VMEM_SPEC
+    out_specs = (HBM_SPEC,) * out_place + (VMEM_SPEC,) * (1 if single else len(outs) - out_place)
     return pl.pallas_call(
         kernel,
         out_shape=outs,
         in_specs=[HBM_SPEC] * in_place + [VMEM_SPEC] * left,
-        out_specs=out_spec if single else (out_spec,) * len(outs),
+        out_specs=out_specs[0] if single else out_specs,
         compiler_params=pltpu.CompilerParams(vmem_limit_bytes=room << 20),
         **options,
     )(
@@ -416,25 +463,18 @@
         block_table.T,
         lengths[None, :],
     )
-    staged, acc, top, totals = call(
-        functools.partial(cached_kernel, page),
-        (shape(new_queries.shape), state, state, state),
-        *cached_inputs,
-        in_place=4,
-        scratch_shapes=[
-            pltpu.VMEM((tokens, columns), jnp.bfloat16),
-            pltpu.VMEM(block_table.shape[::-1], jnp.int32),
-            pltpu.VMEM((1, row_count), jnp.int32),
-            pltpu.VMEM((fresh_count, tokens), jnp.float32),
-            pltpu.VMEM((stack, tokens), jnp.float32),
-            pltpu.SemaphoreType.DMA((4,)),
-        ],
-        room=24,
-    )
+    cached_scratch = [
+        pltpu.VMEM((tokens, columns), jnp.bfloat16),
+        pltpu.VMEM(block_table.shape[::-1], jnp.int32),
+        pltpu.VMEM((1, row_count), jnp.int32),
+        pltpu.VMEM((fresh_count, tokens), jnp.float32),
+        pltpu.VMEM((stack, tokens), jnp.float32),
+        pltpu.SemaphoreType.DMA((4,)),
+    ]
+    cached_types = (shape(new_queries.shape), state, state, state)
     partner_weight = swap(project_weight)
     fresh_type = shape((fresh_count, columns))
     outgoing_type = shape((size, 2, columns))
-    decode_state = (staged, acc, top, totals)
     train_inputs = (train_queries, documents)
     decoded_type, train_type = shape(new_queries.shape), shape(train_queries.shape)
 
@@ -446,47 +486,65 @@
         wide = columns * 3 // 2
 
         others = (1, 2, 3)
-        *slabs, bias, pack = call(
+        staged, acc, top, totals, new_own, train_mine, bias, target, pack = call(
+            functools.partial(paired_cached_kernel, page),
+            cached_types
+            + (
+                shape((row_count, 2, 2 * depth)),
+                shape((train_count, 2 * depth)),
+                shape((1, columns), jnp.float32),
+                shape((1, row_count), jnp.int32),
+                shape(documents.shape, jnp.int32),
+            ),
+            *cached_inputs,
+            new_hidden,
+            train_hidden,
+            project_bias[None, :],
+            destination[None, :],
+            documents,
+            in_place=9,
+            scratch_shapes=cached_scratch + [pltpu.SemaphoreType.DMA((5,))],
+            room=24,
+        )
+        decode_state = (staged, acc, top, totals)
+        slabs = call(
             slab_kernel,
-            (shape((row_count + 1, 2, 2 * depth)),) * 4
-            + (shape((train_count, 2 * depth)),) * 3
-            + (shape((train_count // 2, 2 * depth)),)
-            + (shape((1, columns), jnp.float32), shape(documents.shape, jnp.int32)),
+            (shape((row_count + 1, 2, 2 * depth)),) * 3
+            + (shape((train_count, 2 * depth)),) * 2
+            + (shape((train_count // 2, 2 * depth)),),
             new_hidden,
             train_hidden,
             destination[None, :],
-            project_bias[None, :],
-            documents,
-            in_place=5,
+            in_place=3,
             scratch_shapes=[
                 pltpu.VMEM((1, row_count), jnp.int32),
-                pltpu.SemaphoreType.DMA((11,)),
+                pltpu.SemaphoreType.DMA((7,)),
             ],
         )
-        new_slabs, train_slabs = slabs[:4], slabs[4:]
-        new_rows = [hop(new_slabs[mask], mask) for mask in others]
-        train_rows = [hop(train_slabs[mask], mask) for mask in others]
+        new_rows = [hop(rows, mask) for mask, rows in zip(others, slabs[:3])]
+        train_rows = [hop(rows, mask) for mask, rows in zip(others, slabs[3:])]
         far = lax.ppermute(train_rows[2], "tensor", [(i, i ^ 1) for i in range(beside)])
         weights = (project_weight, partner_weight)
         own_type = shape((fresh_count, columns), jnp.float32)
         sum_type = shape((train_count, columns), jnp.float32)
-        message = fresh_count + 16
+        message = shape((row_count * 3 + 16, columns))
         own, first, second, third, train_own, kept, far_part = call(
             first_product_kernel,
             (
                 own_type,
-                shape((message, wide)),
-                shape((message, wide)),
-                shape((message, wide)),
+                message,
+                message,
+                message,
                 sum_type,
                 shape((16, columns), jnp.float32),
                 shape((train_count, wide)),
             ),
             *weights,
             bias,
-            new_slabs[0],
+            target,
+            new_own,
             *new_rows,
-            train_slabs[0],
+            train_mine,
             train_rows[2],
             far,
         )
@@ -500,23 +558,49 @@
         )
         other = swap(same)
         decoded = call(decode_kernel, decoded_type, fresh, *decode_state)
-        return call(
-            paired_train_kernel,
-            (decoded_type, train_type, outgoing_type),
-            train_queries,
+        decoded, handover, train_own, allowed = call(
+            settle_kernel,
+            (
+                decoded_type,
+                outgoing_type,
+                sum_type,
+                shape((train_count, train_count), jnp.float32),
+            ),
             pack,
             decoded,
             same,
             other,
             train_own,
-            *train_back,
-            out_place=True,
+            train_back[2],
+            out_place=2,
+            scratch_shapes=[
+                pltpu.VMEM((size, 2, columns), jnp.bfloat16),
+                pltpu.SemaphoreType.DMA((2,)),
+            ],
+        )
+        train_attention = call(
+            paired_train_kernel,
+            train_type,
+            train_queries,
+            allowed,
+            train_own,
+            *train_back[:2],
+            out_place=1,
             scratch_shapes=[
                 pltpu.VMEM(train_queries.shape, jnp.bfloat16),
-                pltpu.VMEM((size, 2, columns), jnp.bfloat16),
-                pltpu.SemaphoreType.DMA((2 + local_kv,)),
+                pltpu.SemaphoreType.DMA((local_kv,)),
             ],
         )
+        return (decoded, train_attention, handover)
+
+    decode_state = call(
+        functools.partial(cached_kernel, page),
+        cached_types,
+        *cached_inputs,
+        in_place=4,
+        scratch_shapes=cached_scratch,
+        room=24,
+    )
 
     def gathered(hidden):
         rows = hidden.reshape(-1, chips, 2 * depth)

time: 42.3 us -> 38.8 us (0.917)
  waiting for transfers between devices: 13.1 us -> 9.18 us
  Pallas kernels: 9.12 us -> 9.78 us
    ppermute x12, waiting for transfers between devices: 13.1 us -> 8.83 us  [hop(): return lax.ppermute(value, 'fsdp', [(i, i ^ 2 * mask) for i in range(size)])]
    pallas_call x7 -> x8, Pallas kernels: 9.12 us -> 9.78 us  [call(): pl.pallas_call(kernel, out_shape=outs, in_specs=[HBM_SPEC] * in_place + [...]
  transfers between devices with their start and end apart: 15 -> 15, of which waited for: 4 -> 6; matrix products, arithmetic and copies ran while one was open for 0% -> 0% of each run, Pallas kernels for 18% -> 22%
where the time goes in v3:
time: 38.8 us; the launch traced here: 38.6 us
  starting transfers between devices  18.9 us (49%)
  Pallas kernels  9.78 us (25%)
  waiting for transfers between devices  9.18 us (24%)
  between operations  0.74 us (2%)
    ppermute x12, starting transfers between devices, hop(): return lax.ppermute(value, 'fsdp', [(i, i ^ 2 * mask) for i in range(size)])  16.7 us
    pallas_call x8, Pallas kernels, call(): pl.pallas_call(kernel, out_shape=outs, in_specs=[HBM_SPEC] * in_place + [...  9.78 us
    ppermute x12, waiting for transfers between devices, hop(): return lax.ppermute(value, 'fsdp', [(i, i ^ 2 * mask) for i in range(size)])  8.83 us
    ppermute x1, starting transfers between devices, steps(): lax.ppermute(train_rows[2], 'tensor', [(i, i ^ 1) for i in range(beside)])  1.58 us
  transfers between devices with their start and end apart: 15, of which 6 were waited for; matrix products, arithmetic and copies ran while one was open for 0% of the time, Pallas kernels for 22%

profile of v3, /device:TPU:0, one launch (start us, length us, event | category | flops | bytes accessed | tf_op | source)
XLA Modules:
  0.0 38.6 jit_solution(6778796671860245274)
XLA Ops:
  0.6 0.6 %collective-permute-start = (bf16[1024,512]{1,0:T(8,128)(2,1)}, bf16[1024,512]{1,0:T(8,128)(2,1)S(1)}, u32[]{:S(2)}, u32[]{:S(2)}) collective-permute-start(bf16[1024,512]{1,0:T(8,128)(2,1)} %weight_ref.3), channel_id=1, source_target_pairs={{0,4},{4,0},{8,12},{12,8},{16,20},{20,16},{24,28},{28,24},{1,5},{5... | collective-permute-start | bytes 3145736 | tf_op jit(solution)/shard_map/ppermute | solution.py:448
  1.2 1.3 %shard_map.131 = (bf16[17,2,2048]{2,1,0:T(2,128)(2,1)S(1)}, bf16[17,2,2048]{2,1,0:T(2,128)(2,1)S(1)}, bf16[17,2,2048]{2,1,0:T(2,128)(2,1)S(1)}, bf16[64,2048]{1,...) custom-call(bf16[16,2,8192]{2,1,0:T(2,128)(2,1)} %new_hbm.3, bf16[64,8192]{1,0:T(8,128)(2,1)} %train_hbm.3, ...), custom_call_target="tpu_custom_call" | custom-call | tf_op jit(solution)/shard_map/pallas_call | solution.py:415
  2.5 3.5 %collective-permute-start.4 = (bf16[32,2048]{1,0:T(8,128)(2,1)S(1)}, bf16[32,2048]{1,0:T(8,128)(2,1)S(1)}, u32[]{:S(2)}, u32[]{:S(2)}) collective-permute-start(bf16[32,2048]{1,0:T(8,128)(2,1)S(1)} %get-tuple-element.41), channel_id=1, source_target_pairs={{0,24},{4,28},{8,16},{12,20},{16,8},{20,12},{24,0},{28,4},{1,25},{... | collective-permute-start | bytes 393224 | tf_op jit(solution)/shard_map/ppermute | solution.py:484
  6.1 0.5 %collective-permute-start.1 = (bf16[17,2,2048]{2,1,0:T(2,128)(2,1)S(1)}, bf16[17,2,2048]{2,1,0:T(2,128)(2,1)S(1)}, u32[]{:S(2)}, u32[]{:S(2)}) collective-permute-start(bf16[17,2,2048]{2,1,0:T(2,128)(2,1)S(1)} %get-tuple-element.37), channel_id=1, source_target_pairs={{0,8},{4,12},{8,0},{12,4},{16,24},{20,28},{24,16},{28,20},{1,9},{5... | collective-permute-start | bytes 417800 | tf_op jit(solution)/shard_map/ppermute | solution.py:484
  6.7 1.9 %collective-permute-start.11 = (bf16[64,2048]{1,0:T(8,128)(2,1)S(1)}, bf16[64,2048]{1,0:T(8,128)(2,1)S(1)}, u32[]{:S(2)}, u32[]{:S(2)}) collective-permute-start(bf16[64,2048]{1,0:T(8,128)(2,1)S(1)} %get-tuple-element.58), channel_id=1, source_target_pairs={{0,8},{4,12},{8,0},{12,4},{16,24},{20,28},{24,16},{28,20},{1,9},{5... | collective-permute-start | bytes 786440 | tf_op jit(solution)/shard_map/ppermute | solution.py:484
  8.6 1.8 %collective-permute-done.4.refs_5_ = bf16[32,2048]{1,0:T(8,128)(2,1)S(1)} collective-permute-done((bf16[32,2048]{1,0:T(8,128)(2,1)S(1)}, bf16[32,2048]{1,0:T(8,128)(2,1)S(1)}, u32[]{:S(2)}, u32[]{:S(2)}) %collective-permute-start.4) | collective-permute-done | bytes 131104 | tf_op jit(solution)/shard_map/ppermute | solution.py:484
  10.4 2.0 %collective-permute-start.12 = (bf16[64,2048]{1,0:T(8,128)(2,1)S(1)}, bf16[64,2048]{1,0:T(8,128)(2,1)S(1)}, u32[]{:S(2)}, u32[]{:S(2)}) collective-permute-start(bf16[64,2048]{1,0:T(8,128)(2,1)S(1)} %get-tuple-element.59), channel_id=1, source_target_pairs={{0,16},{4,20},{8,24},{12,28},{16,0},{20,4},{24,8},{28,12},{1,17},{... | collective-permute-start | bytes 786440 | tf_op jit(solution)/shard_map/ppermute | solution.py:484
  12.4 1.5 %collective-permute-done.1.refs_1_ = bf16[17,2,2048]{2,1,0:T(2,128)(2,1)S(1)} collective-permute-done((bf16[17,2,2048]{2,1,0:T(2,128)(2,1)S(1)}, bf16[17,2,2048]{2,1,0:T(2,128)(2,1)S(1)}, u32[]{:S(2)}, u32[]{:S(2)}) %collective-permute-start.1) | collective-permute-done | bytes 139296 | tf_op jit(solution)/shard_map/ppermute | solution.py:484
  14.0 1.4 %collective-permute-start.3 = (bf16[17,2,2048]{2,1,0:T(2,128)(2,1)S(1)}, bf16[17,2,2048]{2,1,0:T(2,128)(2,1)S(1)}, u32[]{:S(2)}, u32[]{:S(2)}) collective-permute-start(bf16[17,2,2048]{2,1,0:T(2,128)(2,1)S(1)} %get-tuple-element.39), channel_id=1, source_target_pairs={{0,24},{4,28},{8,16},{12,20},{16,8},{20,12},{24,0},{28,4},{1,25},{... | collective-permute-start | bytes 417800 | tf_op jit(solution)/shard_map/ppermute | solution.py:484
  15.4 1.6 %collective-permute-start.5 = (bf16[32,2048]{1,0:T(8,128)(2,1)S(1)}, bf16[32,2048]{1,0:T(8,128)(2,1)S(1)}, u32[]{:S(2)}, u32[]{:S(2)}) collective-permute-start(bf16[32,2048]{1,0:T(8,128)(2,1)S(1)} %collective-permute-done.4.refs_5_), channel_id=1, source_target_pairs={{0,1},{1,0},{2,3},{3,2},{4,5},{5,4},{6,7},{7,6},{8,9},{9,8},{10,11... | collective-permute-start | bytes 393224 | tf_op jit(solution)/shard_map/ppermute | solution.py:526
  16.9 4.2 %shard_map.130 = (bf16[16,2,2048]{2,1,0:T(2,128)(2,1)S(1)}, f32[2,256,128]{2,1,0:T(8,128)S(1)}, f32[2,256,128]{2,1,0:T(8,128)S(1)}, f32[2,256,128]{2,1,0:T(8,128...) custom-call(bf16[16,2,2048]{2,1,0:T(2,128)(2,1)} %q_hbm.1, ...), custom_call_target="tpu_custom_call" | custom-call | tf_op jit(solution)/shard_map/pallas_call | solution.py:415
  21.1 0.7 %collective-permute-done.3.refs_3_ = bf16[17,2,2048]{2,1,0:T(2,128)(2,1)S(1)} collective-permute-done((bf16[17,2,2048]{2,1,0:T(2,128)(2,1)S(1)}, bf16[17,2,2048]{2,1,0:T(2,128)(2,1)S(1)}, u32[]{:S(2)}, u32[]{:S(2)}) %collective-permute-start.3) | collective-permute-done | bytes 139296 | tf_op jit(solution)/shard_map/ppermute | solution.py:484
  21.8 0.9 %shard_map.132 = (f32[32,512]{1,0:T(8,128)S(1)}, bf16[64,512]{1,0:T(8,128)(2,1)S(1)}, bf16[64,512]{1,0:T(8,128)(2,1)S(1)}, bf16[64,512]{1,0:T(8,128)(2,1)S(1)}, ...) custom-call(bf16[1024,512]{1,0:T(8,128)(2,1)S(1)} %copy-done, ...), custom_call_target="tpu_custom_call" | custom-call | tf_op jit(solution)/shard_map/pallas_call | solution.py:415
  22.7 1.7 %collective-permute-start.6 = (bf16[64,512]{1,0:T(8,128)(2,1)S(1)}, bf16[64,512]{1,0:T(8,128)(2,1)S(1)}, u32[]{:S(2)}, u32[]{:S(2)}) collective-permute-start(bf16[64,512]{1,0:T(8,128)(2,1)S(1)} %get-tuple-element.44), channel_id=1, source_target_pairs={{0,8},{4,12},{8,0},{12,4},{16,24},{20,28},{24,16},{28,20},{1,9},{5... | collective-permute-start | bytes 196616 | tf_op jit(solution)/shard_map/ppermute | solution.py:484
  24.5 1.5 %collective-permute-start.10 = (bf16[64,768]{1,0:T(8,128)(2,1)S(1)}, bf16[64,768]{1,0:T(8,128)(2,1)S(1)}, u32[]{:S(2)}, u32[]{:S(2)}) collective-permute-start(bf16[64,768]{1,0:T(8,128)(2,1)S(1)} %get-tuple-element.54), channel_id=1, source_target_pairs={{0,24},{4,28},{8,16},{12,20},{16,8},{20,12},{24,0},{28,4},{1,25},{... | collective-permute-start | bytes 294920 | tf_op jit(solution)/shard_map/ppermute | solution.py:484
  26.0 0.5 %shard_map.136 = (bf16[64,768]{1,0:T(8,128)(2,1)S(1)}, bf16[64,768]{1,0:T(8,128)(2,1)S(1)}) custom-call(bf16[1024,512]{1,0:T(8,128)(2,1)S(1)} %copy-done, bf16[1024,512]{1,0:T(8,128)(2,1)S(1)} %collective-permute-done.partner_ref, bf16[64,2048]{1,0:T(8,128)(2,1)S(1)} %collective-permute-done.11.first_ref, bf16[64,2048]{1,0:T(8,128)(2,1)S(1)} %collective-permute-done.12.second_ref), custom_call_target="tpu_custom_call" | custom-call | tf_op jit(solution)/shard_map/pallas_call | solution.py:415
  26.5 1.6 %collective-permute-start.13 = (bf16[64,768]{1,0:T(8,128)(2,1)S(1)}, bf16[64,768]{1,0:T(8,128)(2,1)S(1)}, u32[]{:S(2)}, u32[]{:S(2)}) collective-permute-start(bf16[64,768]{1,0:T(8,128)(2,1)S(1)} %get-tuple-element.60), channel_id=1, source_target_pairs={{0,8},{4,12},{8,0},{12,4},{16,24},{20,28},{24,16},{28,20},{1,9},{5... | collective-permute-start | bytes 294920 | tf_op jit(solution)/shard_map/ppermute | solution.py:484
  28.0 0.5 %collective-permute-start.14 = (bf16[64,768]{1,0:T(8,128)(2,1)S(1)}, bf16[64,768]{1,0:T(8,128)(2,1)S(1)}, u32[]{:S(2)}, u32[]{:S(2)}) collective-permute-start(bf16[64,768]{1,0:T(8,128)(2,1)S(1)} %get-tuple-element.61), channel_id=1, source_target_pairs={{0,16},{4,20},{8,24},{12,28},{16,0},{20,4},{24,8},{28,12},{1,17},{... | collective-permute-start | bytes 294920 | tf_op jit(solution)/shard_map/ppermute | solution.py:484
  28.5 1.6 %collective-permute-start.7 = (bf16[64,512]{1,0:T(8,128)(2,1)S(1)}, bf16[64,512]{1,0:T(8,128)(2,1)S(1)}, u32[]{:S(2)}, u32[]{:S(2)}) collective-permute-start(bf16[64,512]{1,0:T(8,128)(2,1)S(1)} %get-tuple-element.45), channel_id=1, source_target_pairs={{0,16},{4,20},{8,24},{12,28},{16,0},{20,4},{24,8},{28,12},{1,17},{... | collective-permute-start | bytes 196616 | tf_op jit(solution)/shard_map/ppermute | solution.py:484
  30.4 4.0 %collective-permute-done.7.refs_1_ = bf16[64,512]{1,0:T(8,128)(2,1)S(1)} collective-permute-done((bf16[64,512]{1,0:T(8,128)(2,1)S(1)}, bf16[64,512]{1,0:T(8,128)(2,1)S(1)}, u32[]{:S(2)}, u32[]{:S(2)}) %collective-permute-start.7) | collective-permute-done | bytes 65568 | tf_op jit(solution)/shard_map/ppermute | solution.py:484
  34.4 0.8 %collective-permute-done.8.refs_2_ = bf16[64,512]{1,0:T(8,128)(2,1)S(1)} collective-permute-done((bf16[64,512]{1,0:T(8,128)(2,1)S(1)}, bf16[64,512]{1,0:T(8,128)(2,1)S(1)}, u32[]{:S(2)}, u32[]{:S(2)}) %collective-permute-start.8) | collective-permute-done | bytes 65568 | tf_op jit(solution)/shard_map/ppermute | solution.py:484
  35.3 0.8 %shard_map.134.decoded_ref = bf16[16,2,2048]{2,1,0:T(2,128)(2,1)S(1)} custom-call(bf16[32,512]{1,0:T(8,128)(2,1)S(1)} %get-tuple-element.47.fresh_ref, bf16[16,2,2048]{2,1,0:T(2,128)(2,1)S(1)} %get-tuple-element.48.q_ref, f32[2,256,128]{2,1,0:T(8,128)S(1)} %get-tuple-element.49.acc_ref, f32[2,256,128]{2,1,0:T(8,128)S(1)} %get-tuple-element.50.top_ref, ...), custom_call_target="tpu_custom_call" | custom-call | tf_op jit(solution)/shard_map/pallas_call | solution.py:415
  36.5 0.7 %shard_map.135 = (bf16[16,2,2048]{2,1,0:T(2,128)(2,1)}, bf16[8,2,512]{2,1,0:T(2,128)(2,1)}, f32[64,512]{1,0:T(8,128)S(1)}, f32[64,64]{1,0:T(8,128)S(1)}) custom-call(s32[1,64]{1,0:T(1,128)S(1)} %get-tuple-element.33.document_ref, bf16[16,2,2048]{2,1,0:T(2,128)(2,1)S(1)} %shard_map.134.decoded_ref, bf16[16,512]{1,0:T(8,128)(2,1)S(1)} %get-tuple-element.52.same_ref, ...), custom_call_target="tpu_custom_call" | custom-call | tf_op jit(solution)/shard_map/pallas_call | solution.py:415
  37.3 1.4 %shard_map.137 = bf16[64,2048]{1,0:T(8,128)(2,1)} custom-call(bf16[64,2048]{1,0:T(8,128)(2,1)S(1)} %copy-done.1, f32[64,64]{1,0:T(8,128)S(1)} %get-tuple-element.56.allowed_ref, f32[64,512]{1,0:T(8,128)S(1)} %get-tuple-element.57.own_ref, bf16[64,768]{1,0:T(8,128)(2,1)S(1)} %collective-permute-done.13.first_ref, ...), custom_call_target="tpu_custom_call" | custom-call | tf_op jit(solution)/shard_map/pallas_call | solution.py:415
  (18 shorter events, 1.0 us)
Async XLA Ops:
  0.6 21.2 %collective-permute-start = (bf16[1024,512]{1,0:T(8,128)(2,1)}, bf16[1024,512]{1,0:T(8,128)(2,1)S(1)}, u32[]{:S(2)}, u32[]{:S(2)}) collective-permute-start(bf16[1024,512]{1,0:T(8,128)(2,1)} %weight_ref.3), channel_id=1, source_target_pairs={{0,4},{4,0},{8,12},{12,8},{16,20},{20,16},{24,28},{28,24},{1,5},{5... | collective-permute-start | bytes 3145736 | tf_op jit(solution)/shard_map/ppermute | solution.py:448
  2.5 19.3 %copy-start = (bf16[1024,512]{1,0:T(8,128)(2,1)S(1)}, bf16[1024,512]{1,0:T(8,128)(2,1)}, u32[]{:S(2)}) copy-start(bf16[1024,512]{1,0:T(8,128)(2,1)} %weight_ref.3) | copy-start | bytes 3145732
  2.5 7.9 %collective-permute-start.4 = (bf16[32,2048]{1,0:T(8,128)(2,1)S(1)}, bf16[32,2048]{1,0:T(8,128)(2,1)S(1)}, u32[]{:S(2)}, u32[]{:S(2)}) collective-permute-start(bf16[32,2048]{1,0:T(8,128)(2,1)S(1)} %get-tuple-element.41), channel_id=1, source_target_pairs={{0,24},{4,28},{8,16},{12,20},{16,8},{20,12},{24,0},{28,4},{1,25},{... | collective-permute-start | bytes 393224 | tf_op jit(solution)/shard_map/ppermute | solution.py:484
  6.1 7.9 %collective-permute-start.1 = (bf16[17,2,2048]{2,1,0:T(2,128)(2,1)S(1)}, bf16[17,2,2048]{2,1,0:T(2,128)(2,1)S(1)}, u32[]{:S(2)}, u32[]{:S(2)}) collective-permute-start(bf16[17,2,2048]{2,1,0:T(2,128)(2,1)S(1)} %get-tuple-element.37), channel_id=1, source_target_pairs={{0,8},{4,12},{8,0},{12,4},{16,24},{20,28},{24,16},{28,20},{1,9},{5... | collective-permute-start | bytes 417800 | tf_op jit(solution)/shard_map/ppermute | solution.py:484
  6.6 8.8 %collective-permute-start.2 = (bf16[17,2,2048]{2,1,0:T(2,128)(2,1)S(1)}, bf16[17,2,2048]{2,1,0:T(2,128)(2,1)S(1)}, u32[]{:S(2)}, u32[]{:S(2)}) collective-permute-start(bf16[17,2,2048]{2,1,0:T(2,128)(2,1)S(1)} %get-tuple-element.38), channel_id=1, source_target_pairs={{0,16},{4,20},{8,24},{12,28},{16,0},{20,4},{24,8},{28,12},{1,17},{... | collective-permute-start | bytes 417800 | tf_op jit(solution)/shard_map/ppermute | solution.py:484
  6.7 19.3 %collective-permute-start.11 = (bf16[64,2048]{1,0:T(8,128)(2,1)S(1)}, bf16[64,2048]{1,0:T(8,128)(2,1)S(1)}, u32[]{:S(2)}, u32[]{:S(2)}) collective-permute-start(bf16[64,2048]{1,0:T(8,128)(2,1)S(1)} %get-tuple-element.58), channel_id=1, source_target_pairs={{0,8},{4,12},{8,0},{12,4},{16,24},{20,28},{24,16},{28,20},{1,9},{5... | collective-permute-start | bytes 786440 | tf_op jit(solution)/shard_map/ppermute | solution.py:484
  10.4 15.6 %collective-permute-start.12 = (bf16[64,2048]{1,0:T(8,128)(2,1)S(1)}, bf16[64,2048]{1,0:T(8,128)(2,1)S(1)}, u32[]{:S(2)}, u32[]{:S(2)}) collective-permute-start(bf16[64,2048]{1,0:T(8,128)(2,1)S(1)} %get-tuple-element.59), channel_id=1, source_target_pairs={{0,16},{4,20},{8,24},{12,28},{16,0},{20,4},{24,8},{28,12},{1,17},{... | collective-permute-start | bytes 786440 | tf_op jit(solution)/shard_map/ppermute | solution.py:484
  14.0 7.8 %collective-permute-start.3 = (bf16[17,2,2048]{2,1,0:T(2,128)(2,1)S(1)}, bf16[17,2,2048]{2,1,0:T(2,128)(2,1)S(1)}, u32[]{:S(2)}, u32[]{:S(2)}) collective-permute-start(bf16[17,2,2048]{2,1,0:T(2,128)(2,1)S(1)} %get-tuple-element.39), channel_id=1, source_target_pairs={{0,24},{4,28},{8,16},{12,20},{16,8},{20,12},{24,0},{28,4},{1,25},{... | collective-permute-start | bytes 417800 | tf_op jit(solution)/shard_map/ppermute | solution.py:484
  15.4 6.4 %collective-permute-start.5 = (bf16[32,2048]{1,0:T(8,128)(2,1)S(1)}, bf16[32,2048]{1,0:T(8,128)(2,1)S(1)}, u32[]{:S(2)}, u32[]{:S(2)}) collective-permute-start(bf16[32,2048]{1,0:T(8,128)(2,1)S(1)} %collective-permute-done.4.refs_5_), channel_id=1, source_target_pairs={{0,1},{1,0},{2,3},{3,2},{4,5},{5,4},{6,7},{7,6},{8,9},{9,8},{10,11... | collective-permute-start | bytes 393224 | tf_op jit(solution)/shard_map/ppermute | solution.py:526
  22.7 7.4 %collective-permute-start.6 = (bf16[64,512]{1,0:T(8,128)(2,1)S(1)}, bf16[64,512]{1,0:T(8,128)(2,1)S(1)}, u32[]{:S(2)}, u32[]{:S(2)}) collective-permute-start(bf16[64,512]{1,0:T(8,128)(2,1)S(1)} %get-tuple-element.44), channel_id=1, source_target_pairs={{0,8},{4,12},{8,0},{12,4},{16,24},{20,28},{24,16},{28,20},{1,9},{5... | collective-permute-start | bytes 196616 | tf_op jit(solution)/shard_map/ppermute | solution.py:484
  24.5 12.8 %copy-start.1 = (bf16[64,2048]{1,0:T(8,128)(2,1)S(1)}, bf16[64,2048]{1,0:T(8,128)(2,1)}, u32[]{:S(2)}) copy-start(bf16[64,2048]{1,0:T(8,128)(2,1)} %q_ref.1) | copy-start | bytes 786436
  24.5 12.1 %collective-permute-start.10 = (bf16[64,768]{1,0:T(8,128)(2,1)S(1)}, bf16[64,768]{1,0:T(8,128)(2,1)S(1)}, u32[]{:S(2)}, u32[]{:S(2)}) collective-permute-start(bf16[64,768]{1,0:T(8,128)(2,1)S(1)} %get-tuple-element.54), channel_id=1, source_target_pairs={{0,24},{4,28},{8,16},{12,20},{16,8},{20,12},{24,0},{28,4},{1,25},{... | collective-permute-start | bytes 294920 | tf_op jit(solution)/shard_map/ppermute | solution.py:484
  26.5 10.7 %collective-permute-start.13 = (bf16[64,768]{1,0:T(8,128)(2,1)S(1)}, bf16[64,768]{1,0:T(8,128)(2,1)S(1)}, u32[]{:S(2)}, u32[]{:S(2)}) collective-permute-start(bf16[64,768]{1,0:T(8,128)(2,1)S(1)} %get-tuple-element.60), channel_id=1, source_target_pairs={{0,8},{4,12},{8,0},{12,4},{16,24},{20,28},{24,16},{28,20},{1,9},{5... | collective-permute-start | bytes 294920 | tf_op jit(solution)/shard_map/ppermute | solution.py:484
  28.0 9.2 %collective-permute-start.14 = (bf16[64,768]{1,0:T(8,128)(2,1)S(1)}, bf16[64,768]{1,0:T(8,128)(2,1)S(1)}, u32[]{:S(2)}, u32[]{:S(2)}) collective-permute-start(bf16[64,768]{1,0:T(8,128)(2,1)S(1)} %get-tuple-element.61), channel_id=1, source_target_pairs={{0,16},{4,20},{8,24},{12,28},{16,0},{20,4},{24,8},{28,12},{1,17},{... | collective-permute-start | bytes 294920 | tf_op jit(solution)/shard_map/ppermute | solution.py:484
  28.5 5.9 %collective-permute-start.7 = (bf16[64,512]{1,0:T(8,128)(2,1)S(1)}, bf16[64,512]{1,0:T(8,128)(2,1)S(1)}, u32[]{:S(2)}, u32[]{:S(2)}) collective-permute-start(bf16[64,512]{1,0:T(8,128)(2,1)S(1)} %get-tuple-element.45), channel_id=1, source_target_pairs={{0,16},{4,20},{8,24},{12,28},{16,0},{20,4},{24,8},{28,12},{1,17},{... | collective-permute-start | bytes 196616 | tf_op jit(solution)/shard_map/ppermute | solution.py:484
  30.1 5.2 %collective-permute-start.8 = (bf16[64,512]{1,0:T(8,128)(2,1)S(1)}, bf16[64,512]{1,0:T(8,128)(2,1)S(1)}, u32[]{:S(2)}, u32[]{:S(2)}) collective-permute-start(bf16[64,512]{1,0:T(8,128)(2,1)S(1)} %get-tuple-element.46), channel_id=1, source_target_pairs={{0,24},{4,28},{8,16},{12,20},{16,8},{20,12},{24,0},{28,4},{1,25},{... | collective-permute-start | bytes 196616 | tf_op jit(solution)/shard_map/ppermute | solution.py:484
  35.3 1.2 %collective-permute-start.9 = (bf16[16,512]{1,0:T(8,128)(2,1)S(1)}, bf16[16,512]{1,0:T(8,128)(2,1)S(1)}, u32[]{:S(2)}, u32[]{:S(2)}) collective-permute-start(bf16[16,512]{1,0:T(8,128)(2,1)S(1)} %get-tuple-element.52.same_ref), channel_id=1, source_target_pairs={{0,4},{4,0},{8,12},{12,8},{16,20},{20,16},{24,28},{28,24},{1,5},{5... | collective-permute-start | bytes 49160 | tf_op jit(solution)/shard_map/ppermute | solution.py:448
